TPU v7x, 128 devices: a whole 4x4x4 slice. The times are simulated.
128 devices in a mesh: tm: 16 (over z, y), space: 8 (over x, core).
Axes of the slice: x: 4, y: 4, z: 4, core: 2. Of those that a mesh axis runs over, the one named last changes fastest.
Arguments:
- attn_query: bfloat16 [16384, 2560], P(('tm', 'space')), may hold values from -8 to 8
- attn_key: bfloat16 [16384, 2560], P(('tm', 'space')), may hold values from -8 to 8
- attn_value: bfloat16 [16384, 2560], P(('tm', 'space')), may hold values from -6 to 6
- attn_outgrad: bfloat16 [16384, 2560], P(('tm', 'space')), may hold values from -6 to 6
- fast_query: bfloat16 [16384, 1536], P('tm'), may hold values from -6 to 6
- fast_outgrad: bfloat16 [16384, 1536], P('tm'), may hold values from -6 to 6
- fast_key: bfloat16 [16384, 1536], P('tm'), may hold values from -6 to 6
- gate_weights: bfloat16 [16, 1536, 3072], P('tm', None, 'space'), may hold values from -0.15625 to 0.15625
- up_weights: bfloat16 [16, 1536, 3072], P('tm', None, 'space'), may hold values from -0.15625 to 0.15625
- down_weights: bfloat16 [16, 3072, 1536], P('tm', 'space'), may hold values from -0.109375 to 0.109375
- gate_factor: bfloat16 [16384, 3072], P('tm', 'space'), may hold values from -0.15625 to 0.15625
- clip_groups: int32 [4], replicated, may hold values from 1 to 8, 16 in all
Outputs:
- query_grad: bfloat16 [16384, 2560], P(('tm', 'space'))
- key_grad: bfloat16 [16384, 2560], P(('tm', 'space'))
- value_grad: bfloat16 [16384, 2560], P(('tm', 'space'))
- fast_grad: bfloat16 [16384, 1536], P(('tm', 'space'))
- rate_grad: float32 [16384], P(('tm', 'space'))
Inputs may be any that keep to these rules, and one draw needn't show every extreme that they name: `clip_groups`: clip k covers the groups after those of clips 0 to k - 1; the counts sum to 16.
All inputs are finite; a program needn't handle non-finite values.
Results may differ from a plain program's by a relative error of at most 0.012.
Values may be sent and summed in bfloat16 or wider, within the bound.
A program may use at most 192 MiB of HBM per device.

v0:
```python
import math

import jax
import jax.numpy as jnp
from jax import lax
from jax.sharding import Mesh
from jax.sharding import PartitionSpec as P

HEAD = 128
REACH = 64
TM = ("tm_0", "tm_1")
TM_SPACE = ("tm_0", "tm_1", "space")


def extended(array, sides, width):
    for axis, dim in sides:
        devices, length = (lax.axis_size(axis), array.shape[dim])
        up = [(i, (i + 1) % devices) for i in range(devices - 1)]
        down = [(j, i) for i, j in up]
        last = lax.slice_in_dim(array, length - width, length, axis=dim)
        leading = lax.slice_in_dim(array, 0, width, axis=dim)
        before = lax.ppermute(last, axis, up)
        after = lax.ppermute(leading, axis, down)
        array = jnp.concatenate([before, array, after], axis=dim)
    return array


def filled_with(array, identity):
    return jax.tree.map(
        lambda part, zero: jnp.zeros_like(part) + jnp.asarray(zero, part.dtype), array, identity
    )


def carried_in(array, axes, combine, identity):
    before = start = filled_with(array, identity)
    running = array
    for axis in reversed(axes):
        devices, mine = (lax.axis_size(axis), lax.axis_index(axis))
        pieces = jax.tree.map(lambda part: lax.all_gather(part, axis), running)
        inside, running = (start, start)
        for k in reversed(range(devices)):
            passed = k > mine
            running = combine(running, jax.tree.map(lambda part: part[k], pieces))
            inside = jax.tree.map(lambda new, old: jnp.where(passed, new, old), running, inside)
        before = combine(inside, before)
    return before


def window_grads(queries, key_rows, value_rows, out_grad, query_pos, key_pos, key_live):
    head_count = queries.shape[1] // HEAD
    query_heads = queries.reshape(queries.shape[0], head_count, HEAD)
    key_heads = key_rows.reshape(key_rows.shape[0], head_count, HEAD)
    value_heads = value_rows.reshape(value_rows.shape[0], head_count, HEAD)
    grad_heads = out_grad.reshape(out_grad.shape[0], head_count, HEAD)
    scaling = 1.0 / math.sqrt(HEAD)
    scores = (
        jnp.einsum("qhd,khd->hqk", query_heads, key_heads, preferred_element_type=jnp.float32)
        * scaling
    )
    allowed = key_live[None, :] & (jnp.abs(query_pos[:, None] - key_pos[None, :]) <= REACH)
    scores = jnp.where(allowed[None], scores, -1e30)
    peak_score = jnp.max(scores, axis=2, keepdims=True)
    exponent = jnp.exp(scores - peak_score)
    attn_weights = exponent / jnp.sum(exponent, axis=2, keepdims=True)
    weights_b = attn_weights.astype(jnp.bfloat16)
    attn_out = jnp.einsum(
        "hqk,khd->qhd", weights_b, value_heads, preferred_element_type=jnp.float32
    )
    row_delta = jnp.sum(grad_heads.astype(jnp.float32) * attn_out, axis=2)
    value_grad = jnp.einsum(
        "hqk,qhd->khd", weights_b, grad_heads, preferred_element_type=jnp.float32
    )
    weight_grad = jnp.einsum(
        "qhd,khd->hqk", grad_heads, value_heads, preferred_element_type=jnp.float32
    )
    score_grad_b = (attn_weights * (weight_grad - jnp.transpose(row_delta)[:, :, None])).astype(
        jnp.bfloat16
    )
    query_grad = (
        jnp.einsum("hqk,khd->qhd", score_grad_b, key_heads, preferred_element_type=jnp.float32)
        * scaling
    )
    key_grad = (
        jnp.einsum("hqk,qhd->khd", score_grad_b, query_heads, preferred_element_type=jnp.float32)
        * scaling
    )
    return (
        query_grad.reshape(queries.shape[0], -1),
        key_grad.reshape(key_rows.shape[0], -1),
        value_grad.reshape(value_rows.shape[0], -1),
    )


def join_segments(earlier, later):
    marker = jnp.maximum(earlier[0], later[0])
    keep_prev = 1.0 - later[0]
    return (marker, keep_prev * earlier[1] + later[1])


def per_device(
    attn_query,
    attn_key,
    attn_value,
    attn_outgrad,
    fast_query,
    fast_outgrad,
    fast_key,
    gate_weights,
    up_weights,
    down_weights,
    gate_factor,
    clip_groups,
):
    tile_rows = attn_query.shape[0]
    reach_rows = tile_rows // 2
    offset = lax.axis_index("space") * tile_rows
    group_rows = lax.axis_size("space") * tile_rows
    nearby = extended(jnp.stack([attn_query, attn_outgrad]), (("space", 1),), reach_rows)
    farther = extended(jnp.stack([attn_key, attn_value]), (("space", 1),), 2 * reach_rows)
    query_pos = offset - reach_rows + jnp.arange(tile_rows + 2 * reach_rows, dtype=jnp.int32)
    key_pos = offset - 2 * reach_rows + jnp.arange(tile_rows + 4 * reach_rows, dtype=jnp.int32)
    key_live = (key_pos >= 0) & (key_pos < group_rows)
    query_ext, key_ext, value_ext = window_grads(
        nearby[0], farther[0], farther[1], nearby[1], query_pos, key_pos, key_live
    )
    query_grad = query_ext[reach_rows : reach_rows + tile_rows]
    key_grad = key_ext[2 * reach_rows : 2 * reach_rows + tile_rows]
    value_grad = value_ext[2 * reach_rows : 2 * reach_rows + tile_rows]
    contract_rows = (((0,), (0,)), ((), ()))
    contract_last = (((1,), (1,)), ((), ()))
    gate_w = gate_weights[0]
    up_w = up_weights[0]
    down_w = down_weights[0]
    gate_pre = jnp.dot(fast_query, gate_w, preferred_element_type=jnp.float32)
    up_pre = jnp.dot(fast_query, up_w, preferred_element_type=jnp.float32)
    gate_sig = jax.nn.sigmoid(gate_pre)
    gate_act = gate_pre * gate_sig
    hidden_grad = lax.dot_general(
        fast_outgrad, down_w, contract_last, preferred_element_type=jnp.float32
    )
    gate_grad_b = (hidden_grad * up_pre * gate_sig * (1.0 + gate_pre * (1.0 - gate_sig))).astype(
        jnp.bfloat16
    )
    up_grad_b = (hidden_grad * gate_act).astype(jnp.bfloat16)
    input_part = lax.dot_general(
        gate_grad_b, gate_w, contract_last, preferred_element_type=jnp.float32
    ) + lax.dot_general(up_grad_b, up_w, contract_last, preferred_element_type=jnp.float32)
    gate_total = lax.dot_general(
        fast_query, gate_grad_b, contract_rows, preferred_element_type=jnp.float32
    )
    starts = jnp.cumsum(clip_groups) - clip_groups
    marker = jnp.any(starts == lax.axis_index(TM)).astype(jnp.float32)
    element = (marker, (1.0 - marker) * gate_total)
    identity = (jnp.zeros((), jnp.float32), jnp.zeros_like(gate_total))
    carried = carried_in(element, TM, join_segments, identity)
    gate_carry = carried[1].astype(jnp.bfloat16)
    rate_part = (
        jnp.sum(
            jnp.dot(fast_key, gate_carry, preferred_element_type=jnp.float32) * gate_factor, axis=1
        )
        / fast_query.shape[0]
    )
    fast_sum, rate_sum = (
        lax.psum_scatter(input_part, "space", scatter_dimension=0, tiled=True),
        lax.psum_scatter(rate_part, "space", scatter_dimension=0, tiled=True),
    )
    return (
        query_grad.astype(jnp.bfloat16),
        key_grad.astype(jnp.bfloat16),
        value_grad.astype(jnp.bfloat16),
        fast_sum.astype(jnp.bfloat16),
        rate_sum,
    )


def solution(mesh):
    split = Mesh(mesh.devices.reshape(4, 4, mesh.shape["space"]), ("tm_0", "tm_1", "space"))
    return jax.shard_map(
        per_device,
        mesh=split,
        in_specs=(
            P(TM_SPACE, None),
            P(TM_SPACE, None),
            P(TM_SPACE, None),
            P(TM_SPACE, None),
            P(TM, None),
            P(TM, None),
            P(TM, None),
            P(TM, None, "space"),
            P(TM, None, "space"),
            P(TM, "space", None),
            P(TM, "space"),
            P(),
        ),
        out_specs=(
            P(TM_SPACE, None),
            P(TM_SPACE, None),
            P(TM_SPACE, None),
            P(TM_SPACE, None),
            P(TM_SPACE),
        ),
        check_vma=False,
    )
```

profile of v0, /device:TPU:1, one launch (start us, length us, event | category | flops | bytes accessed | tf_op | source)
XLA Modules:
  0.0 270.3 jit_solution(16294177592355741497)
XLA Ops:
  9.0 1.3 compare_reduce_fusion
  11.0 4.4 %fusion.17 = f32[1024,384]{1,0:T(8,128)} fusion(bf16[1024,1536]{1,0:T(8,128)(2,1)S(1)} %copy-done, bf16[1,1536,384]{2,1,0:T(8,128)(2,1)} %param.19), kind=kOutput, calls=%fused_computation.41 | convolution fusion | flops 1207959552 | bytes 5898240 | tf_op jit(solution)/shard_map/dot_general | solution.py:134
  15.5 3.0 %fusion.21 = f32[1024,384]{1,0:T(8,128)} fusion(bf16[1024,1536]{1,0:T(8,128)(2,1)S(1)} %copy-done.23, bf16[1,384,1536]{2,1,0:T(8,128)(2,1)S(1)} %copy-done.24), kind=kOutput, calls=%fused_computation.45 | convolution fusion | flops 1207959552 | bytes 5898240 | tf_op jit(solution)/shard_map/dot_general | solution.py:138
  18.4 4.3 %multiply_convert_fusion.4 = bf16[1024,384]{1,0:T(8,128)(2,1)S(1)} fusion(f32[1024,384]{1,0:T(8,128)} %fusion.17, f32[1024,384]{1,0:T(8,128)} %fusion.21, bf16[1024,1536]{1,0:T(8,128)(2,1)S(1)} %copy-done, bf16[1,1536,384]{2,1,0:T(8,128)(2,1)} %param.20), kind=kOutput, calls=%fused_computation.32 | convolution fusion | flops 1211891712 | bytes 8257536 | tf_op jit(solution)/shard_map/dot_general | solution.py:135
  23.6 2.8 %fusion.6 = f32[1536,384]{0,1:T(8,128)} fusion(bf16[1024,384]{1,0:T(8,128)(2,1)S(1)} %multiply_convert_fusion.4, bf16[1024,1536]{1,0:T(8,128)(2,1)S(1)} %copy-done, f32[]{:T(128)S(6)} %sub.109), kind=kOutput, calls=%fused_computation.14 | convolution fusion | flops 1208549376 | bytes 6291460 | tf_op jit(solution)/shard_map/dot_general | solution.py:148
  26.5 3.5 %fusion.15 = f32[1024,1536]{1,0:T(8,128)S(1)} fusion(bf16[1024,384]{1,0:T(8,128)(2,1)} %copy-done.18, bf16[1,1536,384]{2,1,0:T(8,128)(2,1)} %param.19), kind=kOutput, calls=%fused_computation.39 | convolution fusion | flops 1207959552 | bytes 8257536 | tf_op jit(solution)/shard_map/dot_general | solution.py:145
  30.1 4.5 %convolution_add_fusion = f32[1024,1536]{1,0:T(8,128)} fusion(f32[1024,1536]{1,0:T(8,128)S(1)} %fusion.15, bf16[1,1536,384]{2,1,0:T(8,128)(2,1)S(1)} %copy-done.19, f32[1024,384]{1,0:T(8,128)S(1)} %copy-done.17, f32[1024,384]{1,0:T(8,128)S(1)} %copy-done.16), kind=kOutput, calls=%fused_computation.5 | convolution fusion | flops 1211891712 | bytes 16908288 | tf_op jit(solution)/shard_map/dot_general | solution.py:147
  36.5 9.9 %all-reduce = f32[4]{0:T(128)S(1)} all-reduce(f32[4]{0:T(128)S(1)} %dynamic-update-slice), channel_id=1, replica_groups=mesh['tm_0'=4,'tm_1'=4,'space'=8] {'tm_1'}, use_global_device_ids=true, to_apply=%add | all-reduce | flops 4 | bytes 32
  49.5 72.1 %all-gather.6.cloned.1.call-done = f32[6144,384]{0,1:T(8,128)} async-done(((f32[1536,384]{0,1:T(8,128)}), f32[6144,384]{0,1:T(8,128)}) %all-gather.6.cloned.1.call-update) | async-done | bytes 9437200 | tf_op jit(solution)/shard_map/all_gather | solution.py:39
  121.6 4.8 %fusion.8 = f32[1,1536,384]{1,2,0:T(8,128)S(1)} fusion(f32[6144,384]{0,1:T(8,128)} %all-gather.6.cloned.1.call-done, f32[]{:T(128)S(6)} %sub.105, f32[]{:T(128)S(6)} %sub.106, f32[]{:T(128)} %bitcast.33, f32[]{:T(128)S(6)} %sub.107), kind=kLoop, calls=%fused_computation.20 | loop fusion | flops 4128768 | bytes 11796496 | tf_op jit(solution)/shard_map/add | solution.py:97
  126.5 2.1 copy.50
  128.6 1.1 copy-done.20
  130.4 1.2 pad_maximum_fusion.3
  131.5 2.7 %collective-permute-start.1 = (bf16[2,128,2560]{1,2,0:T(8,128)(2,1)}, bf16[2,128,2560]{1,2,0:T(8,128)(2,1)}, u32[]{:S(2)}, u32[]{:S(2)}) collective-permute-start(bf16[2,128,2560]{1,2,0:T(8,128)(2,1)} %pad_maximum_fusion.3), channel_id=1, source_target_pairs={{1,0},{2,1},{3,2},{4,3},{5,4},{6,5},{7,6},{9,8},{10,9},{11,10},{12... | collective-permute-start | bytes 3932168 | tf_op jit(solution)/shard_map/ppermute | solution.py:23
  134.3 3.0 %collective-permute-start = (bf16[2,128,2560]{1,2,0:T(8,128)(2,1)}, bf16[2,128,2560]{1,2,0:T(8,128)(2,1)}, u32[]{:S(2)}, u32[]{:S(2)}) collective-permute-start(bf16[2,128,2560]{1,2,0:T(8,128)(2,1)} %pad_maximum_fusion.3), channel_id=1, source_target_pairs={{0,1},{1,2},{2,3},{3,4},{4,5},{5,6},{6,7},{8,9},{9,10},{10,11},{11... | collective-permute-start | bytes 3932168 | tf_op jit(solution)/shard_map/ppermute | solution.py:22
  137.6 1.7 copy.40
  139.4 1.5 slice_maximum_fusion
  140.9 1.8 copy.43
  142.8 2.4 collective-permute-start.3
  149.5 3.2 %collective-permute-start.2 = (bf16[2,64,2560]{2,1,0:T(8,128)(2,1)S(1)}, bf16[2,64,2560]{2,1,0:T(8,128)(2,1)S(1)}, u32[]{:S(2)}, u32[]{:S(2)}) collective-permute-start(bf16[2,64,2560]{2,1,0:T(8,128)(2,1)S(1)} %copy.42), channel_id=1, source_target_pairs={{0,1},{1,2},{2,3},{3,4},{4,5},{5,6},{6,7},{8,9},{9,10},{10,11},{11... | collective-permute-start | bytes 1966088 | tf_op jit(solution)/shard_map/ppermute | solution.py:22
  152.7 10.1 %all-reduce.1 = f32[4]{0:T(128)S(1)} all-reduce(f32[4]{0:T(128)S(1)} %dynamic-update-slice.1), channel_id=1, replica_groups=mesh['tm_0'=4,'tm_1'=4,'space'=8] {'tm_0'}, use_global_device_ids=true, to_apply=%add.1 | all-reduce | flops 4 | bytes 32
  162.8 2.3 copy.55
  170.0 2.3 copy.45
  172.3 1.4 copy.44
  173.7 3.5 %pad_maximum_fusion.1 = bf16[2,256,2560]{1,2,0:T(8,128)(2,1)S(1)} fusion(bf16[2,64,2560]{1,2,0:T(8,128)(2,1)} %copy.45, bf16[1,128,2560]{1,2,0:T(8,128)(2,1)} %bitcast.102, bf16[1,128,2560]{1,2,0:T(8,128)(2,1)} %bitcast.104, bf16[2,64,2560]{1,2,0:T(8,128)(2,1)} %copy.44), kind=kLoop, calls=%fused_computation.15 | loop fusion | flops 10485760 | bytes 5242880 | tf_op jit(solution)/shard_map/concatenate | solution.py:24
  177.3 1.7 fusion.42
  179.0 2.0 pad_maximum_fusion
  181.0 1.7 fusion.41
  182.7 7.2 %fusion.45 = (f32[20,256]{1,0:T(8,128)S(1)}, f32[20,256,384]{2,1,0:T(8,128)}) fusion(pred[256,384]{1,0:T(8,128)(4,1)S(1)} %fusion.35, bf16[256,20,128]{0,2,1:T(8,128)(2,1)} %bitcast.108, bf16[384,20,128]{0,2,1:T(8,128)(2,1)S(1)} %bitcast.95), kind=kOutput, calls=%fused_computation.74 | convolution fusion | flops 511181184 | bytes 11259904 | tf_op jit(solution)/shard_map/sub | solution.py:63
  190.0 4.0 %fusion.5 = bf16[20,256,384]{2,1,0:T(8,128)(2,1)S(1)} fusion(f32[20,256,384]{2,1,0:T(8,128)} %get-tuple-element.39, f32[20,256]{1,0:T(8,128)S(1)} %get-tuple-element.38), kind=kLoop, calls=%fused_computation.12 | loop fusion | flops 3932160 | bytes 11816960 | tf_op jit(solution)/shard_map/convert_element_type | solution.py:65
  194.4 1.4 fusion.7
  196.0 2.1 copy-done.5
  198.1 2.6 multiply_convert_fusion
  200.8 1.4 fusion.13
  203.0 1.1 copy.56
  204.1 3.0 %fusion.11 = bf16[384,20,128]{0,2,1:T(8,128)(2,1)S(1)} fusion(bf16[256,20,128]{0,2,1:T(8,128)(2,1)S(1)} %bitcast.109, bf16[20,256,384]{2,1,0:T(8,128)(2,1)} %copy-done.2), kind=kOutput, calls=%fused_computation.28 | convolution fusion | flops 505282560 | bytes 7208960 | tf_op jit(solution)/shard_map/hqk,qhd->khd/dot_general | solution.py:84
  207.2 1.1 copy.57
  208.3 3.0 %convert_bitcast_fusion = bf16[384,20,128]{0,2,1:T(8,128)(2,1)S(1)} fusion(bf16[256,20,128]{0,2,1:T(8,128)(2,1)S(1)} %bitcast.107, bf16[20,256,384]{2,1,0:T(8,128)(2,1)} %copy-done.3), kind=kOutput, calls=%fused_computation.27 | convolution fusion | flops 504299520 | bytes 7208960 | tf_op jit(solution)/shard_map/hqk,qhd->khd/dot_general | solution.py:70
  211.4 1.1 copy.58
  212.5 1.9 convert_element_type.47
  214.4 7.4 %all-gather.4.cloned.1.call-done = f32[4,1536,384]{2,1,0:T(8,128)} async-done(((f32[1,1536,384]{2,1,0:T(8,128)}), f32[4,1536,384]{2,1,0:T(8,128)}) %all-gather.4.cloned.1.call-update) | async-done | bytes 9437200 | tf_op jit(solution)/shard_map/all_gather | solution.py:39
  221.9 6.8 %fusion.40 = (f32[1,1536,384]{2,1,0:T(8,128)S(1)}, f32[1,1536,384]{2,1,0:T(8,128)}, f32[1,1536,384]{2,1,0:T(8,128)}, f32[1,1536,384]{2,1,0:T(8,128)}) fusion(f32[4,1536,384]{2,1,0:T(8,128)} %all-gather.4.cloned.1.call-done), kind=kLoop, calls=%fused_computation.69 | loop fusion | bytes 18874368 | tf_op jit(solution)/shard_map/slice | solution.py:43
  228.7 3.1 %copy.66 = f32[1,1536,384]{1,2,0:T(8,128)} copy(f32[1,1536,384]{2,1,0:T(8,128)} %get-tuple-element.23) | data formatting | bytes 4718592
  231.8 3.1 %copy.65 = f32[1,1536,384]{1,2,0:T(8,128)} copy(f32[1,1536,384]{2,1,0:T(8,128)} %get-tuple-element.21) | data formatting | bytes 4718592
  234.9 3.0 %copy.64 = f32[1,1536,384]{1,2,0:T(8,128)} copy(f32[1,1536,384]{2,1,0:T(8,128)} %get-tuple-element.22) | data formatting | bytes 4718592
  238.0 2.1 copy.63
  240.1 9.6 %fusion.12 = f32[1024]{0:T(1024)S(1)} fusion(bf16[1024,384]{0,1:T(8,128)(2,1)} %copy.55, bf16[1024,1536]{1,0:T(8,128)(2,1)} %param.18, f32[1,1536,384]{1,2,0:T(8,128)} %copy-done.4, f32[1,1536,384]{1,2,0:T(8,128)} %copy.66, f32[1,1536,384]{1,2,0:T(8,128)} %copy.65, f32[1,1536,384]{1,2,0:T(8,128)} %copy.64, f32[1,1536,384]{1,2,0:T(8,128)} %copy.63, ...), kind=kOutput, calls=%fused_computation.30 | convolution fusion | flops 1222704128 | bytes 22813204 | tf_op jit(solution)/shard_map/dot_general | solution.py:159
  249.7 12.6 %all-reduce.2 = f32[1024]{0:T(1024)S(1)} all-reduce(f32[1024]{0:T(1024)S(1)} %broadcast_multiply_fusion), channel_id=4, replica_groups=mesh['tm_0'=4,'tm_1'=4,'space'=8] {'space'}, use_global_device_ids=true, to_apply=%region_7.8.clone | all-reduce | flops 1024 | bytes 8192
  (88 shorter events, 11.4 us)
Async XLA Ops:
  8.0 3.0 %copy-start = (bf16[1024,1536]{1,0:T(8,128)(2,1)S(1)}, bf16[1024,1536]{1,0:T(8,128)(2,1)}, u32[]{:S(2)}) copy-start(bf16[1024,1536]{1,0:T(8,128)(2,1)} %param.16) | copy-start | bytes 9437188
  8.0 113.6 %all-gather.6.cloned.1.call-start = ((), (), s32[]{:S(2)}) async-start(), calls=%async_computation.3 | async-start | bytes 11796480 | tf_op jit(solution)/shard_map/all_gather | solution.py:39
  11.0 4.5 %copy-start.23 = (bf16[1024,1536]{1,0:T(8,128)(2,1)S(1)}, bf16[1024,1536]{1,0:T(8,128)(2,1)}, u32[]{:S(2)}) copy-start(bf16[1024,1536]{1,0:T(8,128)(2,1)} %param.17) | copy-start | bytes 9437188
  11.0 4.5 %copy-start.24 = (bf16[1,384,1536]{2,1,0:T(8,128)(2,1)S(1)}, bf16[1,384,1536]{2,1,0:T(8,128)(2,1)}, u32[]{:S(2)}) copy-start(bf16[1,384,1536]{2,1,0:T(8,128)(2,1)} %param.21) | copy-start | bytes 3538948
  22.7 0.9 copy-start.18
  26.5 3.6 %copy-start.16 = (f32[1024,384]{1,0:T(8,128)S(1)}, f32[1024,384]{1,0:T(8,128)}, u32[]{:S(2)}) copy-start(f32[1024,384]{1,0:T(8,128)} %fusion.17) | copy-start | bytes 4718596
  26.5 3.6 %copy-start.17 = (f32[1024,384]{1,0:T(8,128)S(1)}, f32[1024,384]{1,0:T(8,128)}, u32[]{:S(2)}) copy-start(f32[1024,384]{1,0:T(8,128)} %fusion.21) | copy-start | bytes 4718596
  26.5 186.0 %reduce-scatter.2.cloned.1.call-start = ((), (), s32[]{:S(2)}) async-start(), calls=%async_computation.1 | async-start | bytes 7077888 | tf_op jit(solution)/shard_map/reduce_scatter | solution.py:164
  26.5 3.5 %copy-start.19 = (bf16[1,1536,384]{2,1,0:T(8,128)(2,1)S(1)}, bf16[1,1536,384]{2,1,0:T(8,128)(2,1)}, u32[]{:S(2)}) copy-start(bf16[1,1536,384]{2,1,0:T(8,128)(2,1)} %param.20) | copy-start | bytes 3538948
  34.5 0.7 copy-start.27
  34.6 187.3 %all-gather.4.cloned.1.call-start = ((), (), s32[]{:S(2)}) async-start(), calls=%async_computation.2 | async-start | bytes 11796480 | tf_op jit(solution)/shard_map/all_gather | solution.py:39
  126.5 2.1 copy-start.4
  128.6 1.1 copy-start.20
  128.6 1.4 copy-start.21
  130.0 7.6 %copy-start.6 = (bf16[128,2560]{0,1:T(8,128)(2,1)}, bf16[128,2560]{0,1:T(8,128)(2,1)S(1)}, u32[]{:S(2)}) copy-start(bf16[128,2560]{0,1:T(8,128)(2,1)S(1)} %copy.39) | copy-start | bytes 1966084
  130.0 7.3 %copy-start.22 = (bf16[128,2560]{1,0:T(8,128)(2,1)S(1)}, bf16[128,2560]{1,0:T(8,128)(2,1)}, u32[]{:S(2)}) copy-start(bf16[128,2560]{1,0:T(8,128)(2,1)} %param.15) | copy-start | bytes 1966084
  130.3 9.0 %copy-start.8 = (bf16[128,2560]{0,1:T(8,128)(2,1)}, bf16[128,2560]{0,1:T(8,128)(2,1)S(1)}, u32[]{:S(2)}) copy-start(bf16[128,2560]{0,1:T(8,128)(2,1)S(1)} %copy.38) | copy-start | bytes 1966084
  131.5 47.4 %collective-permute-start.1 = (bf16[2,128,2560]{1,2,0:T(8,128)(2,1)}, bf16[2,128,2560]{1,2,0:T(8,128)(2,1)}, u32[]{:S(2)}, u32[]{:S(2)}) collective-permute-start(bf16[2,128,2560]{1,2,0:T(8,128)(2,1)} %pad_maximum_fusion.3), channel_id=1, source_target_pairs={{1,0},{2,1},{3,2},{4,3},{5,4},{6,5},{7,6},{9,8},{10,9},{11,10},{12... | collective-permute-start | bytes 3932168 | tf_op jit(solution)/shard_map/ppermute | solution.py:23
  134.3 44.6 %collective-permute-start = (bf16[2,128,2560]{1,2,0:T(8,128)(2,1)}, bf16[2,128,2560]{1,2,0:T(8,128)(2,1)}, u32[]{:S(2)}, u32[]{:S(2)}) collective-permute-start(bf16[2,128,2560]{1,2,0:T(8,128)(2,1)} %pad_maximum_fusion.3), channel_id=1, source_target_pairs={{0,1},{1,2},{2,3},{3,4},{4,5},{5,6},{6,7},{8,9},{9,10},{10,11},{11... | collective-permute-start | bytes 3932168 | tf_op jit(solution)/shard_map/ppermute | solution.py:22
  137.6 3.3 %copy-start.10 = (bf16[128,2560]{0,1:T(8,128)(2,1)}, bf16[128,2560]{0,1:T(8,128)(2,1)S(1)}, u32[]{:S(2)}) copy-start(bf16[128,2560]{0,1:T(8,128)(2,1)S(1)} %copy.41) | copy-start | bytes 1966084
  139.4 3.4 %copy-start.11 = (bf16[128,2560]{0,1:T(8,128)(2,1)}, bf16[128,2560]{0,1:T(8,128)(2,1)S(1)}, u32[]{:S(2)}) copy-start(bf16[128,2560]{0,1:T(8,128)(2,1)S(1)} %copy.40) | copy-start | bytes 1966084
  140.9 7.2 %copy-start.26 = (u32[128]{0:T(128)S(1)}, u32[128]{0:T(128)}, u32[]{:S(2)}) copy-start(u32[128]{0:T(128)} %constant.76) | copy-start | bytes 1540
  142.7 26.0 %copy-start.25 = (u32[128]{0:T(128)S(1)}, u32[128]{0:T(128)}, u32[]{:S(2)}) copy-start(u32[128]{0:T(128)} %constant.83) | copy-start | bytes 1540
  142.8 27.2 %collective-permute-start.3 = (bf16[2,64,2560]{2,1,0:T(8,128)(2,1)S(1)}, bf16[2,64,2560]{2,1,0:T(8,128)(2,1)}, u32[]{:S(2)}, u32[]{:S(2)}) collective-permute-start(bf16[2,64,2560]{2,1,0:T(8,128)(2,1)S(1)} %copy.43), channel_id=1, source_target_pairs={{1,0},{2,1},{3,2},{4,3},{5,4},{6,5},{7,6},{9,8},{10,9},{11,10},{12... | collective-permute-start | bytes 1966088 | tf_op jit(solution)/shard_map/ppermute | solution.py:23
  149.5 22.8 %collective-permute-start.2 = (bf16[2,64,2560]{2,1,0:T(8,128)(2,1)S(1)}, bf16[2,64,2560]{2,1,0:T(8,128)(2,1)S(1)}, u32[]{:S(2)}, u32[]{:S(2)}) collective-permute-start(bf16[2,64,2560]{2,1,0:T(8,128)(2,1)S(1)} %copy.42), channel_id=1, source_target_pairs={{0,1},{1,2},{2,3},{3,4},{4,5},{5,6},{6,7},{8,9},{9,10},{10,11},{11... | collective-permute-start | bytes 1966088 | tf_op jit(solution)/shard_map/ppermute | solution.py:22
  177.2 1.7 copy-start.7
  177.2 1.8 copy-start.9
  190.0 4.1 %copy-start.12 = (bf16[1,256,2560]{1,2,0:T(8,128)(2,1)S(1)}, bf16[1,256,2560]{1,2,0:T(8,128)(2,1)}, u32[]{:S(2)}) copy-start(bf16[1,256,2560]{1,2,0:T(8,128)(2,1)} %get-tuple-element.27) | copy-start | bytes 3932164
  190.0 4.4 %copy-start.15 = (bf16[1,384,2560]{1,2,0:T(8,128)(2,1)S(1)}, bf16[1,384,2560]{1,2,0:T(8,128)(2,1)}, u32[]{:S(2)}) copy-start(bf16[1,384,2560]{1,2,0:T(8,128)(2,1)} %get-tuple-element.24) | copy-start | bytes 5898244
  190.0 8.2 %copy-start.5 = (f32[20,256,384]{2,1,0:T(8,128)S(1)}, f32[20,256,384]{2,1,0:T(8,128)}, u32[]{:S(2)}) copy-start(f32[20,256,384]{2,1,0:T(8,128)} %get-tuple-element.39) | copy-start | bytes 23592964
  194.0 2.0 copy-start.3
  200.8 1.9 copy-start.2
  202.7 1.4 copy-start.14
  207.0 1.3 copy-start.13
  240.1 22.8 %copy-start.1 = (bf16[1024,1536]{1,0:T(8,128)(2,1)S(1)}, bf16[1024,1536]{1,0:T(8,128)(2,1)}, u32[]{:S(2)}) copy-start(bf16[1024,1536]{1,0:T(8,128)(2,1)} %param.16) | copy-start | bytes 9437188
Sparse Core Ops, SparseCore 0:
  26.6 94.9 all-gather.5
  128.7 93.0 all-gather.3
Sparse Core Ops, SparseCore 1:
  34.6 45.1 reduce-scatter.1
where the time goes:
time: 272 us; the launch traced here: 270 us
  waiting for transfers between devices  79.6 us (29%)
  matrix products  50.6 us (19%)
  local copies, waits for them, and re-layouts  49.7 us (18%)
  blocking collectives  32.7 us (12%)
  between operations  24.8 us (9%)
  other arithmetic  21.6 us (8%)
  starting transfers between devices  11.4 us (4%)
    all_gather x2, waiting for transfers between devices, carried_in(): pieces = jax.tree.map(lambda part: lax.all_gather(part, axis), running)  79.6 us
    unnamed x3, blocking collectives  32.7 us
    unnamed x76, local copies, waits for them, and re-layouts  29.6 us
    dot_general x1, matrix products, per_device(): jnp.dot(fast_key, gate_carry, preferred_element_type=jnp.float32)  9.56 us
    slice x3, local copies, waits for them, and re-layouts, carried_in(): running = combine(running, jax.tree.map(lambda part: part[k], pieces))  8.1 us
    sub x1, matrix products, window_grads(): exponent = jnp.exp(scores - peak_score)  7.23 us
    ppermute x2, starting transfers between devices, extended(): before = lax.ppermute(last, axis, up)  6.16 us
    concatenate x2, other arithmetic, extended(): array = jnp.concatenate([before, array, after], axis=dim)  5.57 us
  transfers between devices with their start and end apart: 7, of which 2 were waited for; matrix products, arithmetic and copies ran while one was open for 26% of the time, Pallas kernels for 0%

commit v1 on v0

v1 whole, which is shorter than its diff:
```python
import functools
import math

import jax
import jax.numpy as jnp
from jax import lax
from jax.experimental import pallas as pl
from jax.experimental.pallas import tpu as pltpu
from jax.sharding import PartitionSpec as P

MESH = pl.DeviceIdType.MESH
F32 = jnp.float32
BF16 = jnp.bfloat16

HEAD = 128
REACH = 64
NT = (((1,), (1,)), ((), ()))
TN = (((0,), (0,)), ((), ()))
ORDER = (10, 2, 8, 6, 14, 9, 11, 5, 15, 7, 13, 1, 3, 4, 12)


def kernel(
    clips, aq, ak, av, ao, fq, fo, fk, wg, wu, wd, gf,
    o_q, o_k, o_v, o_f, o_r,
    q_b, o_b, k_b, w_b, wd_b, f_b, aq_b, ao_b, kx, vx,
    gu, g_t, gtot, rx, cout, cin, ip, prx, psum, rsx,
    dq, dk_f, dv_f, dkv_s, dkv_r, f_t, bias, rate_s, rate_r, rate_o, fast_o, dk_o, dv_o,
    ld, halo_s, halo_r, a1_s, a1_r, a2_s, a2_r, pr_s, pr_r, rs_s, rs_r, dk_s, dk_r, rt_s, rt_r, st,
):
    tm, sp = lax.axis_index("tm"), lax.axis_index("space")
    mz, my = tm // 4, tm % 4
    mx, mk = sp // 2, sp % 2
    rows, hid = gf.shape
    feat = fq.shape[1]
    half = feat // 2
    tile = aq.shape[0]
    blk = hid // 8
    rt = 256

    barrier = pltpu.get_barrier_semaphore()
    for j in range(1, 16):
        pl.semaphore_signal(barrier, inc=1, device_id={"tm": lax.rem(tm + j, 16)}, device_id_type=MESH)
    for j in range(1, 8):
        pl.semaphore_signal(barrier, inc=1, device_id={"space": lax.rem(sp + j, 8)}, device_id_type=MESH)

    def load(i, src, dst):
        return pltpu.make_async_copy(src, dst, ld.at[i])

    first = [
        load(0, wg.at[0], w_b.at[:, pl.ds(0, hid)]),
        load(1, wu.at[0], w_b.at[:, pl.ds(hid, hid)]),
        load(2, fq, q_b),
        load(3, wd.at[0], wd_b),
        load(4, fo, o_b),
    ]
    later = [
        load(5, aq, aq_b),
        load(6, ao, ao_b),
        load(7, ak, kx.at[pl.ds(REACH, tile)]),
        load(8, av, vx.at[pl.ds(REACH, tile)]),
        load(9, fk, k_b),
        load(10, gf, f_b),
    ]
    for c in first:
        c.start()
    for c in later:
        c.start()

    left, right = lax.rem(sp + 7, 8), lax.rem(sp + 1, 8)

    def halo(i, src, dst, to):
        return pltpu.make_async_remote_copy(
            src_ref=src, dst_ref=dst, send_sem=halo_s.at[i], recv_sem=halo_r.at[i],
            device_id={"space": to}, device_id_type=MESH,
        )

    halos = [
        halo(0, ak.at[pl.ds(0, REACH)], kx.at[pl.ds(REACH + tile, REACH)], left),
        halo(1, av.at[pl.ds(0, REACH)], vx.at[pl.ds(REACH + tile, REACH)], left),
        halo(2, ak.at[pl.ds(tile - REACH, REACH)], kx.at[pl.ds(0, REACH)], right),
        halo(3, av.at[pl.ds(tile - REACH, REACH)], vx.at[pl.ds(0, REACH)], right),
    ]
    pl.semaphore_wait(barrier, 22)
    for c in halos:
        c.start()

    for c in first:
        c.wait()

    def rows_step(r, _):
        at = pl.ds(pl.multiple_of(r * rt, rt), rt)
        pre = jnp.dot(q_b[at, :], w_b[...], preferred_element_type=F32)
        hg = lax.dot_general(o_b[at, :], wd_b[...], NT, preferred_element_type=F32)
        gate, up = pre[:, :hid], pre[:, hid:]
        sig = 1.0 / (1.0 + jnp.exp(-gate))
        g = (hg * up * sig * (1.0 + gate * (1.0 - sig))).astype(BF16)
        gu[at, pl.ds(0, hid)] = g
        gu[at, pl.ds(hid, hid)] = (hg * (gate * sig)).astype(BF16)
        g_t[:, at] = g.T
        return 0

    lax.fori_loop(0, rows // rt, rows_step, 0)

    for h in range(2):
        def total_step(n, _):
            at = pl.ds(pl.multiple_of(n * 256, 256), 256)
            src = pl.ds(pl.multiple_of(h * half + n * 256, 256), 256)
            gtot[h, :, at] = jnp.dot(g_t[...], q_b[:, src], preferred_element_type=F32).astype(BF16)
            return 0

        lax.fori_loop(0, half // 256, total_step, 0)

    def peer(kk):
        dz, dy = kk // 4, kk % 4
        return lax.rem(mz + dz, 4) * 4 + lax.rem(my + dy, 4)

    def slice_of(ref, d):
        return ref.at[lax.rem(d, 2), pl.ds(pl.multiple_of((d // 2) * blk, 16), blk)]

    def out_copy(kk):
        d = peer(kk)
        return pltpu.make_async_remote_copy(
            src_ref=slice_of(gtot, d), dst_ref=rx.at[tm], send_sem=a1_s.at[kk], recv_sem=a1_r.at[kk],
            device_id={"tm": d}, device_id_type=MESH,
        )

    for kk in ORDER:
        out_copy(kk).start()
    rx[tm] = gtot[lax.rem(tm, 2), pl.ds(pl.multiple_of((tm // 2) * blk, 16), blk), :]

    def partner_copy(x):
        return pltpu.make_async_remote_copy(
            src_ref=ip.at[pl.ds(pl.multiple_of(x * 2 * tile + (1 - mk) * tile, tile), tile)], dst_ref=prx.at[x],
            send_sem=pr_s.at[x], recv_sem=pr_r.at[x],
            device_id={"space": mx * 2 + 1 - mk}, device_id_type=MESH,
        )

    def input_step(i, _):
        x = lax.rem(mx + 2 + i, 4)
        at = pl.ds(pl.multiple_of(x * rt, rt), rt)
        part = lax.dot_general(gu[at, :], w_b[...], NT, preferred_element_type=F32)
        ip[at, :] = part.astype(BF16)
        partner_copy(x).start()
        return 0

    lax.fori_loop(0, 4, input_step, 0)

    def rs_copy(dd):
        x = lax.rem(mx + dd, 4)
        return pltpu.make_async_remote_copy(
            src_ref=psum.at[x], dst_ref=rsx.at[dd], send_sem=rs_s.at[dd], recv_sem=rs_r.at[dd],
            device_id={"space": x * 2 + mk}, device_id_type=MESH,
        )

    def own_part(x):
        return ip[pl.ds(pl.multiple_of(x * 2 * tile + mk * tile, tile), tile), :].astype(F32)

    for dd in (2, 1, 3):
        x = lax.rem(mx + dd, 4)
        partner_copy(x).wait_recv()
        psum[x] = (own_part(x) + prx[x].astype(F32)).astype(BF16)
        rs_copy(dd).start()

    for c in later[:4]:
        c.wait()
    for c in halos:
        c.wait()
    key = lax.broadcasted_iota(jnp.int32, (2 * tile, tile), 0)
    query = lax.broadcasted_iota(jnp.int32, (2 * tile, tile), 1)
    apart = key - query
    place = key + (sp * tile - REACH)
    allowed = (apart >= 0) & (apart <= 2 * REACH) & (place >= 0) & (place < rows)
    bias[...] = jnp.where(allowed, 0.0, -1e30)
    scaling = 1.0 / math.sqrt(HEAD)

    def head_step(hh, _):
        at = pl.ds(pl.multiple_of(hh * HEAD, HEAD), HEAD)
        q, g, k, v = aq_b[:, at], ao_b[:, at], kx[:, at], vx[:, at]
        s = lax.dot_general(k, q, NT, preferred_element_type=F32) * scaling + bias[...]
        e = jnp.exp(s - jnp.max(s, axis=0, keepdims=True))
        p = e * (1.0 / jnp.sum(e, axis=0, keepdims=True))
        pb = p.astype(BF16)
        dp = lax.dot_general(v, g, NT, preferred_element_type=F32)
        delta = jnp.sum(pb.astype(F32) * dp, axis=0, keepdims=True)
        ds = (p * (dp - delta)).astype(BF16)
        dv = jnp.dot(pb, g, preferred_element_type=F32)
        dk = jnp.dot(ds, q, preferred_element_type=F32) * scaling
        dq[:, at] = (lax.dot_general(ds, k, TN, preferred_element_type=F32) * scaling).astype(BF16)
        dk_f[:, at] = dk[REACH : REACH + tile]
        dv_f[:, at] = dv[REACH : REACH + tile]
        dkv_s[0, 0, :, at] = dk[:REACH].astype(BF16)
        dkv_s[0, 1, :, at] = dv[:REACH].astype(BF16)
        dkv_s[1, 0, :, at] = dk[REACH + tile :].astype(BF16)
        dkv_s[1, 1, :, at] = dv[REACH + tile :].astype(BF16)
        return 0

    lax.fori_loop(0, aq.shape[1] // HEAD, head_step, 0)

    def back(i, to):
        return pltpu.make_async_remote_copy(
            src_ref=dkv_s.at[i], dst_ref=dkv_r.at[i], send_sem=dk_s.at[i], recv_sem=dk_r.at[i],
            device_id={"space": to}, device_id_type=MESH,
        )

    backs = [back(0, left), back(1, right)]
    for c in backs:
        c.start()
    store_q = pltpu.make_async_copy(dq, o_q, st.at[0])
    store_q.start()

    for c in later[4:]:
        c.wait()

    def turn_step(r, _):
        at = pl.ds(pl.multiple_of(r * rt, rt), rt)
        f_t[:, at] = f_b[at, :].T
        return 0

    lax.fori_loop(0, rows // rt, turn_step, 0)

    for kk in ORDER:
        out_copy(kk).wait_recv()
    s1 = clips[0]
    s2 = s1 + clips[1]
    s3 = s2 + clips[2]

    def scan_step(i, carry):
        c = 15 - i
        cout[c] = carry.astype(BF16)
        starts = (c == 0) | (c == s1) | (c == s2) | (c == s3)
        keep = jnp.where(starts, 0.0, 1.0).astype(F32)
        return keep * (carry + rx[c].astype(F32))

    lax.fori_loop(0, 16, scan_step, jnp.zeros((blk, half), F32))

    def carry_copy(kk):
        d = peer(kk)
        return pltpu.make_async_remote_copy(
            src_ref=cout.at[d], dst_ref=slice_of(cin, tm), send_sem=a2_s.at[kk], recv_sem=a2_r.at[kk],
            device_id={"tm": d}, device_id_type=MESH,
        )

    for kk in ORDER:
        carry_copy(kk).start()
    cin[lax.rem(tm, 2), pl.ds(pl.multiple_of((tm // 2) * blk, 16), blk), :] = cout[tm]

    partner_copy(mx).wait_recv()
    total = own_part(mx) + prx[mx].astype(F32)
    for dd in (1, 3, 2):
        rs_copy(dd).wait_recv()
        total = total + rsx[dd].astype(F32)
    fast_o[...] = total.astype(BF16)
    store_f = pltpu.make_async_copy(fast_o, o_f, st.at[1])
    store_f.start()

    for c in backs:
        c.wait_recv()
    dk_o[pl.ds(0, REACH), :] = (dk_f[pl.ds(0, REACH), :] + dkv_r[1, 0].astype(F32)).astype(BF16)
    dk_o[pl.ds(tile - REACH, REACH), :] = (dk_f[pl.ds(tile - REACH, REACH), :] + dkv_r[0, 0].astype(F32)).astype(BF16)
    dv_o[pl.ds(0, REACH), :] = (dv_f[pl.ds(0, REACH), :] + dkv_r[1, 1].astype(F32)).astype(BF16)
    dv_o[pl.ds(tile - REACH, REACH), :] = (dv_f[pl.ds(tile - REACH, REACH), :] + dkv_r[0, 1].astype(F32)).astype(BF16)
    store_k = pltpu.make_async_copy(dk_o, o_k, st.at[2])
    store_v = pltpu.make_async_copy(dv_o, o_v, st.at[3])
    store_k.start()
    store_v.start()

    for kk in ORDER:
        carry_copy(kk).wait_recv()

    def rate_step(r, _):
        at = pl.ds(pl.multiple_of(r * rt, rt), rt)
        kc = lax.dot_general(cin[0], k_b[at, pl.ds(0, half)], NT, preferred_element_type=F32)
        kc += lax.dot_general(cin[1], k_b[at, pl.ds(half, half)], NT, preferred_element_type=F32)
        line = jnp.sum(kc * f_t[:, at].astype(F32), axis=0, keepdims=True) * (1.0 / rows)
        rate_s[2 * r] = jnp.broadcast_to(line[:, :tile], (8, tile))
        rate_s[2 * r + 1] = jnp.broadcast_to(line[:, tile:], (8, tile))
        return 0

    lax.fori_loop(0, rows // rt, rate_step, 0)

    def rate_copy(j):
        d = lax.rem(sp + j, 8)
        return pltpu.make_async_remote_copy(
            src_ref=rate_s.at[d], dst_ref=rate_r.at[j], send_sem=rt_s.at[j], recv_sem=rt_r.at[j],
            device_id={"space": d}, device_id_type=MESH,
        )

    for j in range(1, 8):
        rate_copy(j).start()
    rate = rate_s[sp]
    for j in range(1, 8):
        rate_copy(j).wait_recv()
        rate = rate + rate_r[j]
    rate_o[...] = rate[0:1, :]
    store_r = pltpu.make_async_copy(rate_o, o_r, st.at[4])
    store_r.start()

    for kk in ORDER:
        out_copy(kk).wait_send()
        carry_copy(kk).wait_send()
    for x in range(4):
        partner_copy(x).wait_send()
    for dd in (1, 2, 3):
        rs_copy(dd).wait_send()
    for c in backs:
        c.wait_send()
    for j in range(1, 8):
        rate_copy(j).wait_send()
    for c in (store_q, store_f, store_k, store_v, store_r):
        c.wait()


def per_device(attn_query, attn_key, attn_value, attn_outgrad, fast_query, fast_outgrad, fast_key,
               gate_weights, up_weights, down_weights, gate_factor, clip_groups):
    tile, width = attn_query.shape
    rows, hid = gate_factor.shape
    feat = fast_query.shape[1]
    half, blk = feat // 2, hid // 8
    any_spec = pl.BlockSpec(memory_space=pl.ANY)
    dma = pltpu.SemaphoreType.DMA
    V = pltpu.VMEM
    outs = pl.pallas_call(
        kernel,
        out_shape=(
            jax.ShapeDtypeStruct((tile, width), BF16),
            jax.ShapeDtypeStruct((tile, width), BF16),
            jax.ShapeDtypeStruct((tile, width), BF16),
            jax.ShapeDtypeStruct((tile, feat), BF16),
            jax.ShapeDtypeStruct((1, tile), F32),
        ),
        in_specs=[pl.BlockSpec(memory_space=pltpu.SMEM)] + [any_spec] * 11,
        out_specs=(any_spec,) * 5,
        scratch_shapes=[
            V((rows, feat), BF16), V((rows, feat), BF16), V((rows, feat), BF16),
            V((feat, 2 * hid), BF16), V((hid, feat), BF16), V((rows, hid), BF16),
            V((tile, width), BF16), V((tile, width), BF16), V((2 * tile, width), BF16), V((2 * tile, width), BF16),
            V((rows, 2 * hid), BF16), V((hid, rows), BF16), V((2, hid, half), BF16),
            V((16, blk, half), BF16), V((16, blk, half), BF16), V((2, hid, half), BF16),
            V((rows, feat), BF16), V((4, tile, feat), BF16), V((4, tile, feat), BF16), V((4, tile, feat), BF16),
            V((tile, width), BF16), V((tile, width), F32), V((tile, width), F32),
            V((2, 2, REACH, width), BF16), V((2, 2, REACH, width), BF16),
            V((hid, rows), BF16), V((2 * tile, tile), F32),
            V((8, 8, tile), F32), V((8, 8, tile), F32), V((1, tile), F32),
            V((tile, feat), BF16), V((tile, width), BF16), V((tile, width), BF16),
            dma((11,)), dma((4,)), dma((4,)), dma((16,)), dma((16,)), dma((16,)), dma((16,)),
            dma((4,)), dma((4,)), dma((4,)), dma((4,)), dma((2,)), dma((2,)), dma((8,)), dma((8,)), dma((5,)),
        ],
        compiler_params=pltpu.CompilerParams(
            collective_id=0, has_side_effects=True, vmem_limit_bytes=60 * 1024 * 1024
        ),
    )(clip_groups, attn_query, attn_key, attn_value, attn_outgrad, fast_query, fast_outgrad, fast_key,
      gate_weights, up_weights, down_weights, gate_factor)
    return outs[0], outs[1], outs[2], outs[3], outs[4].reshape(tile)


def solution(mesh):
    both = ("tm", "space")
    return jax.shard_map(
        per_device,
        mesh=mesh,
        in_specs=(
            P(both, None), P(both, None), P(both, None), P(both, None),
            P("tm", None), P("tm", None), P("tm", None),
            P("tm", None, "space"), P("tm", None, "space"), P("tm", "space", None),
            P("tm", "space"), P(),
        ),
        out_specs=(P(both, None), P(both, None), P(both, None), P(both, None), P(both)),
        check_vma=False,
    )
```

time: 272 us -> 66.2 us (0.24)
  waiting for transfers between devices: 79.6 us -> 0 us
  Pallas kernels: 0 us -> 58.1 us
  matrix products: 50.6 us -> 0 us
  local copies, waits for them, and re-layouts: 49.7 us -> 7.21 us
  blocking collectives: 32.7 us -> 0 us
  between operations: 24.8 us -> 0.66 us
  other arithmetic: 21.6 us -> 0 us
  starting transfers between devices: 11.4 us -> 0 us
    all_gather x2 -> x0, waiting for transfers between devices: 79.6 us -> none  [carried_in(): pieces = jax.tree.map(lambda part: lax.all_gather(part, axis), running)]
    pallas_call x0 -> x1, Pallas kernels: none -> 58.1 us  [per_device(): pl.pallas_call(kernel, out_shape=(jax.ShapeDtypeStruct((tile, width), BF1...]
    dot_general x12 -> x0, matrix products: 43.3 us -> none  [the longest x1 9.56 us: per_device(): jnp.dot(fast_key, gate_carry, preferred_element_type=jnp.float32)]
    unnamed x3 -> x0, blocking collectives: 32.7 us -> none
    unnamed x76 -> x9, local copies, waits for them, and re-layouts: 29.6 us -> 7.21 us
    slice x10 -> x0, local copies, waits for them, and re-layouts: 14.3 us -> none  [the longest x3 8.1 us: carried_in(): running = combine(running, jax.tree.map(lambda part: part[k], pieces))]
    ppermute x4 -> x0, starting transfers between devices: 11.3 us -> none  [the longest x2 6.16 us: extended(): before = lax.ppermute(last, axis, up)]
    sub x1 -> x0, matrix products: 7.23 us -> none  [window_grads(): exponent = jnp.exp(scores - peak_score)]
  transfers between devices with their start and end apart: 7 -> 0, of which waited for: 2 -> 0; matrix products, arithmetic and copies ran while one was open for 26% -> 0% of each run, Pallas kernels for 0% -> 0%
where the time goes in v1:
time: 66.2 us; the launch traced here: 65.9 us
  Pallas kernels  58.1 us (88%)
  local copies, waits for them, and re-layouts  7.21 us (11%)
    pallas_call x1, Pallas kernels, per_device(): pl.pallas_call(kernel, out_shape=(jax.ShapeDtypeStruct((tile, width), BF1...  58.1 us
    unnamed x9, local copies, waits for them, and re-layouts  7.21 us

profile of v1, /device:TPU:1, one launch (start us, length us, event | category | flops | bytes accessed | tf_op | source)
XLA Modules:
  0.0 65.9 jit_solution(2522590620974628289)
XLA Ops:
  0.6 58.1 %shard_map.155 = (bf16[128,2560]{1,0:T(8,128)(2,1)}, bf16[128,2560]{1,0:T(8,128)(2,1)}, bf16[128,2560]{1,0:T(8,128)(2,1)}, bf16[128,1536]{1,0:T(8,128)(2,1)}, f32[1,128]{1,0:T(1,128)}) custom-call(s32[4]{0:T(128)} %clips.1, bf16[128,2560]{1,0:T(8,128)(2,1)} %aq.1, bf16[128,2560]{1,0:T(8,128)(2,1)} %ak.1, bf16[128,2560]{1,0:T(8,128)(2,1)} %av.1, ...), custom_call_target="tpu_custom_call" | custom-call | tf_op jit(solution)/shard_map/pallas_call | solution.py:322
  58.7 0.0 copy-start
  58.7 0.0 copy-start.1
  58.7 2.0 %copy.22 = bf16[128,2560]{1,0:T(8,128)(2,1)} copy(bf16[128,2560]{1,0:T(8,128)(2,1)} %get-tuple-element.20) | data formatting | bytes 1310720
  60.8 2.0 %copy.23 = bf16[128,2560]{1,0:T(8,128)(2,1)} copy(bf16[128,2560]{1,0:T(8,128)(2,1)} %get-tuple-element.21) | data formatting | bytes 1310720
  62.7 2.0 %copy.24 = bf16[128,2560]{1,0:T(8,128)(2,1)} copy(bf16[128,2560]{1,0:T(8,128)(2,1)} %get-tuple-element.22) | data formatting | bytes 1310720
  64.7 0.0 copy-done
  64.7 0.7 %copy.25 = bf16[128,1536]{1,0:T(8,128)(2,1)} copy(bf16[128,1536]{1,0:T(8,128)(2,1)S(1)} %copy-done) | data formatting | bytes 786432
  65.4 0.0 copy-done.1
  65.4 0.5 copy.26
Async XLA Ops:
  58.7 6.0 %copy-start = (bf16[128,1536]{1,0:T(8,128)(2,1)S(1)}, bf16[128,1536]{1,0:T(8,128)(2,1)}, u32[]{:S(2)}) copy-start(bf16[128,1536]{1,0:T(8,128)(2,1)} %get-tuple-element.23) | copy-start | bytes 1179652
  58.7 6.7 %copy-start.1 = (f32[1,128]{1,0:T(1,128)S(1)}, f32[1,128]{1,0:T(1,128)}, u32[]{:S(2)}) copy-start(f32[1,128]{1,0:T(1,128)} %get-tuple-element.14) | copy-start | bytes 1540

commit v2 on v1

v2 whole, which is shorter than its diff:
```python
import functools
import math

import jax
import jax.numpy as jnp
from jax import lax
from jax.experimental import pallas as pl
from jax.experimental.pallas import tpu as pltpu
from jax.sharding import PartitionSpec as P

MESH = pl.DeviceIdType.MESH
F32 = jnp.float32
UNROLL = 2
BF16 = jnp.bfloat16

HEAD = 128
REACH = 64
NT = (((1,), (1,)), ((), ()))
TN = (((0,), (0,)), ((), ()))
ORDER = (10, 2, 8, 6, 14, 9, 11, 5, 15, 7, 13, 1, 3, 4, 12)


def kernel(
    clips, aq, ak, av, ao, fq, fo, fk, wg, wu, wd, gf,
    o_q, o_k, o_v, o_f, o_r,
    q_b, o_b, k_b, w_b, wd_b, f_b, aq_b, ao_b, kx, vx,
    gu, g_t, gtot, rx, cout, cin, ip, prx, psum, rsx,
    dk_f, dv_f, dkv_s, dkv_r, f_t, bias, rate_s, rate_r, line,
    ld, halo_s, halo_r, a1_s, a1_r, a2_s, a2_r, pr_s, pr_r, rs_s, rs_r, dk_s, dk_r, rt_s, rt_r,
):
    tm, sp = lax.axis_index("tm"), lax.axis_index("space")
    mz, my = tm // 4, tm % 4
    mx, mk = sp // 2, sp % 2
    rows, hid = gf.shape
    feat = fq.shape[1]
    half = feat // 2
    tile = aq.shape[0]
    blk = hid // 8
    quarter = half // 2
    rt = 256

    barrier = pltpu.get_barrier_semaphore()
    for j in range(1, 16):
        pl.semaphore_signal(barrier, inc=1, device_id={"tm": lax.rem(tm + j, 16)}, device_id_type=MESH)
    for j in range(1, 8):
        pl.semaphore_signal(barrier, inc=1, device_id={"space": lax.rem(sp + j, 8)}, device_id_type=MESH)

    def load(i, src, dst):
        return pltpu.make_async_copy(src, dst, ld.at[i])

    weights = [
        load(0, wg.at[0], w_b.at[:, pl.ds(0, hid)]),
        load(1, wu.at[0], w_b.at[:, pl.ds(hid, hid)]),
        load(2, wd.at[0], wd_b),
    ]

    def block(r):
        return pl.ds(pl.multiple_of(r * rt, rt), rt)

    def inputs(r):
        return [
            load(3 + r, fq.at[block(r)], q_b.at[block(r)]),
            load(7 + r, fo.at[block(r)], o_b.at[block(r)]),
        ]

    later = [
        load(11, aq, aq_b),
        load(12, ao, ao_b),
        load(13, ak, kx.at[pl.ds(REACH, tile)]),
        load(14, av, vx.at[pl.ds(REACH, tile)]),
        load(15, fk, k_b),
        load(16, gf, f_b),
    ]
    for c in weights:
        c.start()
    for r in range(4):
        for c in inputs(r):
            c.start()

    left, right = lax.rem(sp + 7, 8), lax.rem(sp + 1, 8)

    def halo(i, src, dst, to):
        return pltpu.make_async_remote_copy(
            src_ref=src, dst_ref=dst, send_sem=halo_s.at[i], recv_sem=halo_r.at[i],
            device_id={"space": to}, device_id_type=MESH,
        )

    halos = [
        halo(0, ak.at[pl.ds(0, REACH)], kx.at[pl.ds(REACH + tile, REACH)], left),
        halo(1, av.at[pl.ds(0, REACH)], vx.at[pl.ds(REACH + tile, REACH)], left),
        halo(2, ak.at[pl.ds(tile - REACH, REACH)], kx.at[pl.ds(0, REACH)], right),
        halo(3, av.at[pl.ds(tile - REACH, REACH)], vx.at[pl.ds(0, REACH)], right),
    ]
    pl.semaphore_wait(barrier, 22)
    for c in halos:
        c.start()

    def peer(kk):
        dz, dy = kk // 4, kk % 4
        return lax.rem(mz + dz, 4) * 4 + lax.rem(my + dy, 4)

    def slice_of(ref, n, d):
        down, over = pl.multiple_of((d // 2) * blk, 16), pl.multiple_of(lax.rem(d, 2) * quarter, 128)
        return ref.at[n, pl.ds(down, blk), pl.ds(over, quarter)]

    def out_copy(n, kk):
        d = peer(kk)
        return pltpu.make_async_remote_copy(
            src_ref=slice_of(gtot, n, d), dst_ref=rx.at[n, tm],
            send_sem=a1_s.at[n * 16 + kk], recv_sem=a1_r.at[n * 16 + kk],
            device_id={"tm": d}, device_id_type=MESH,
        )

    def carry_copy(n, kk):
        d = peer(kk)
        return pltpu.make_async_remote_copy(
            src_ref=cout.at[n, d], dst_ref=slice_of(cin, n, tm),
            send_sem=a2_s.at[n * 16 + kk], recv_sem=a2_r.at[n * 16 + kk],
            device_id={"tm": d}, device_id_type=MESH,
        )

    for c in weights:
        c.wait()

    def rows_step(r, _):
        at = block(r)
        for c in inputs(r):
            c.wait()
        pre = jnp.dot(q_b[at, :], w_b[...], preferred_element_type=F32)
        hg = lax.dot_general(o_b[at, :], wd_b[...], NT, preferred_element_type=F32)
        gate, up = pre[:, :hid], pre[:, hid:]
        sig = 1.0 / (1.0 + jnp.exp(-gate))
        g = (hg * up * sig * (1.0 + gate * (1.0 - sig))).astype(BF16)
        gu[at, pl.ds(0, hid)] = g
        gu[at, pl.ds(hid, hid)] = (hg * (gate * sig)).astype(BF16)
        g_t[:, at] = g.T
        return 0

    lax.fori_loop(0, rows // rt, rows_step, 0)
    for c in later:
        c.start()

    for n in range(2):
        def total_step(i, _, n=n):
            at = pl.ds(pl.multiple_of(i * 256, 256), 256)
            src = pl.ds(pl.multiple_of(n * half + i * 256, 256), 256)
            gtot[n, :, at] = jnp.dot(g_t[...], q_b[:, src], preferred_element_type=F32).astype(BF16)
            return 0

        lax.fori_loop(0, half // 256, total_step, 0)
        for kk in ORDER:
            out_copy(n, kk).start()
        rx[n, tm] = slice_of(gtot, n, tm)[...]

    s1 = clips[0]
    s2 = s1 + clips[1]
    s3 = s2 + clips[2]

    def carries(n):
        for kk in ORDER:
            out_copy(n, kk).wait_recv()

        def scan_step(i, carry):
            c = 15 - i
            cout[n, c] = carry.astype(BF16)
            starts = (c == 0) | (c == s1) | (c == s2) | (c == s3)
            keep = jnp.where(starts, 0.0, 1.0).astype(F32)
            return keep * (carry + rx[n, c].astype(F32))

        lax.fori_loop(0, 16, scan_step, jnp.zeros((blk, quarter), F32))
        for kk in ORDER:
            carry_copy(n, kk).start()
        slice_of(cin, n, tm)[...] = cout[n, tm]

    def partner_copy(x):
        return pltpu.make_async_remote_copy(
            src_ref=ip.at[pl.ds(pl.multiple_of(x * 2 * tile + (1 - mk) * tile, tile), tile)], dst_ref=prx.at[x],
            send_sem=pr_s.at[x], recv_sem=pr_r.at[x],
            device_id={"space": mx * 2 + 1 - mk}, device_id_type=MESH,
        )

    def input_step(i, _):
        x = lax.rem(mx + 2 + i, 4)
        at = pl.ds(pl.multiple_of(x * rt, rt), rt)
        terms = lax.dot_general(gu[at, :], w_b[...], NT, preferred_element_type=F32)
        ip[at, :] = terms.astype(BF16)
        partner_copy(x).start()
        return 0

    lax.fori_loop(0, 4, input_step, 0)

    ahead, behind = 1 + 2 * mk, 3 - 2 * mk

    def rs_copy(i, to):
        return pltpu.make_async_remote_copy(
            src_ref=psum.at[i], dst_ref=rsx.at[i], send_sem=rs_s.at[i], recv_sem=rs_r.at[i],
            device_id={"space": lax.rem(mx + to, 4) * 2 + mk}, device_id_type=MESH,
        )

    relay = [rs_copy(0, ahead), rs_copy(1, ahead), rs_copy(2, behind)]

    def pair_sum(to):
        x = lax.rem(mx + to, 4)
        partner_copy(x).wait_recv()
        mine = ip[pl.ds(pl.multiple_of(x * 2 * tile + mk * tile, tile), tile), :]
        return mine.astype(F32) + prx[x].astype(F32)

    psum[0] = pair_sum(2).astype(BF16)
    relay[0].start()
    psum[2] = pair_sum(behind).astype(BF16)
    relay[2].start()

    for c in later[:4]:
        c.wait()
    for c in halos:
        c.wait()
    key = lax.broadcasted_iota(jnp.int32, (2 * tile, tile), 0)
    query = lax.broadcasted_iota(jnp.int32, (2 * tile, tile), 1)
    apart = key - query
    place = key + (sp * tile - REACH)
    allowed = (apart >= 0) & (apart <= 2 * REACH) & (place >= 0) & (place < rows)
    bias[...] = jnp.where(allowed, 0.0, -1e30)
    scaling = 1.0 / math.sqrt(HEAD)

    def one_head(hh):
        at = pl.ds(pl.multiple_of(hh * HEAD, HEAD), HEAD)
        q, g, k, v = aq_b[:, at], ao_b[:, at], kx[:, at], vx[:, at]
        s = lax.dot_general(k, q, NT, preferred_element_type=F32) * (scaling * math.log2(math.e)) + bias[...]
        e = jnp.exp2(s - jnp.max(s, axis=0, keepdims=True))
        p = e * (1.0 / jnp.sum(e, axis=0, keepdims=True))
        pb = p.astype(BF16)
        dp = lax.dot_general(v, g, NT, preferred_element_type=F32)
        delta = jnp.sum(pb.astype(F32) * dp, axis=0, keepdims=True)
        ds = (p * (dp - delta)).astype(BF16)
        dv = jnp.dot(pb, g, preferred_element_type=F32)
        dk = jnp.dot(ds, q, preferred_element_type=F32) * scaling
        o_q[:, at] = (lax.dot_general(ds, k, TN, preferred_element_type=F32) * scaling).astype(BF16)
        dk_f[:, at] = dk[REACH : REACH + tile]
        dv_f[:, at] = dv[REACH : REACH + tile]
        dkv_s[0, 0, :, at] = dk[:REACH].astype(BF16)
        dkv_s[0, 1, :, at] = dv[:REACH].astype(BF16)
        dkv_s[1, 0, :, at] = dk[REACH + tile :].astype(BF16)
        dkv_s[1, 1, :, at] = dv[REACH + tile :].astype(BF16)

    def head_step(i, _):
        for j in range(UNROLL):
            one_head(i * UNROLL + j)
        return 0

    steps = aq.shape[1] // HEAD // UNROLL
    lax.fori_loop(0, steps // 2, head_step, 0)
    relay[0].wait_recv()
    psum[1] = (pair_sum(ahead) + rsx[0].astype(F32)).astype(BF16)
    relay[1].start()
    carries(0)
    lax.fori_loop(steps // 2, steps, head_step, 0)

    def back(i, to):
        return pltpu.make_async_remote_copy(
            src_ref=dkv_s.at[i], dst_ref=dkv_r.at[i], send_sem=dk_s.at[i], recv_sem=dk_r.at[i],
            device_id={"space": to}, device_id_type=MESH,
        )

    backs = [back(0, left), back(1, right)]
    for c in backs:
        c.start()

    for c in later[4:]:
        c.wait()

    def turn_step(r, _):
        at = pl.ds(pl.multiple_of(r * rt, rt), rt)
        f_t[:, at] = f_b[at, :].T
        return 0

    lax.fori_loop(0, rows // rt, turn_step, 0)

    carries(1)

    total = pair_sum(0)
    for i in (2, 1):
        relay[i].wait_recv()
        total = total + rsx[i].astype(F32)
    o_f[...] = total.astype(BF16)

    for c in backs:
        c.wait_recv()
    o_k[pl.ds(0, REACH), :] = (dk_f[pl.ds(0, REACH), :] + dkv_r[1, 0].astype(F32)).astype(BF16)
    o_k[pl.ds(tile - REACH, REACH), :] = (dk_f[pl.ds(tile - REACH, REACH), :] + dkv_r[0, 0].astype(F32)).astype(BF16)
    o_v[pl.ds(0, REACH), :] = (dv_f[pl.ds(0, REACH), :] + dkv_r[1, 1].astype(F32)).astype(BF16)
    o_v[pl.ds(tile - REACH, REACH), :] = (dv_f[pl.ds(tile - REACH, REACH), :] + dkv_r[0, 1].astype(F32)).astype(BF16)

    for n in range(2):
        for kk in ORDER:
            carry_copy(n, kk).wait_recv()

        def rate_step(r, _, n=n):
            at = block(r)
            kc = lax.dot_general(cin[n], k_b[at, pl.ds(n * half, half)], NT, preferred_element_type=F32)
            more = jnp.sum(kc * f_t[:, at].astype(F32), axis=0, keepdims=True)
            if n == 0:
                line[r] = more
            else:
                more = (line[r] + more) * (1.0 / rows)
                rate_s[2 * r] = jnp.broadcast_to(more[:, :tile], (8, tile))
                rate_s[2 * r + 1] = jnp.broadcast_to(more[:, tile:], (8, tile))
            return 0

        lax.fori_loop(0, rows // rt, rate_step, 0)

    def rate_copy(j):
        d = lax.rem(sp + j, 8)
        return pltpu.make_async_remote_copy(
            src_ref=rate_s.at[d], dst_ref=rate_r.at[j], send_sem=rt_s.at[j], recv_sem=rt_r.at[j],
            device_id={"space": d}, device_id_type=MESH,
        )

    for j in range(1, 8):
        rate_copy(j).start()
    rate = rate_s[sp]
    for j in range(1, 8):
        rate_copy(j).wait_recv()
        rate = rate + rate_r[j]
    o_r[...] = rate[0:1, :]

    for kk in ORDER:
        for n in range(2):
            out_copy(n, kk).wait_send()
            carry_copy(n, kk).wait_send()
    for x in range(4):
        partner_copy(x).wait_send()
    for c in relay:
        c.wait_send()
    for c in backs:
        c.wait_send()
    for j in range(1, 8):
        rate_copy(j).wait_send()


def put_out(a, b, c, d, e, oa, ob, oc, od, oe, sem):
    copies = [pltpu.make_async_copy(src, dst, sem.at[i])
              for i, (src, dst) in enumerate(((a, oa), (b, ob), (c, oc), (d, od), (e, oe)))]
    for c in copies:
        c.start()
    for c in copies:
        c.wait()


def per_device(attn_query, attn_key, attn_value, attn_outgrad, fast_query, fast_outgrad, fast_key,
               gate_weights, up_weights, down_weights, gate_factor, clip_groups):
    tile, width = attn_query.shape
    rows, hid = gate_factor.shape
    feat = fast_query.shape[1]
    half, blk = feat // 2, hid // 8
    any_spec = pl.BlockSpec(memory_space=pl.ANY)
    dma = pltpu.SemaphoreType.DMA
    V = pltpu.VMEM
    outs = pl.pallas_call(
        kernel,
        out_shape=(
            V((tile, width), BF16), V((tile, width), BF16), V((tile, width), BF16),
            V((tile, feat), BF16), V((1, tile), F32),
        ),
        in_specs=[pl.BlockSpec(memory_space=pltpu.SMEM)] + [any_spec] * 11,
        out_specs=(pl.BlockSpec(memory_space=V),) * 5,
        scratch_shapes=[
            V((rows, feat), BF16), V((rows, feat), BF16), V((rows, feat), BF16),
            V((feat, 2 * hid), BF16), V((hid, feat), BF16), V((rows, hid), BF16),
            V((tile, width), BF16), V((tile, width), BF16), V((2 * tile, width), BF16), V((2 * tile, width), BF16),
            V((rows, 2 * hid), BF16), V((hid, rows), BF16), V((2, hid, half), BF16),
            V((2, 16, blk, half // 2), BF16), V((2, 16, blk, half // 2), BF16), V((2, hid, half), BF16),
            V((rows, feat), BF16), V((4, tile, feat), BF16), V((3, tile, feat), BF16), V((3, tile, feat), BF16),
            V((tile, width), F32), V((tile, width), F32),
            V((2, 2, REACH, width), BF16), V((2, 2, REACH, width), BF16),
            V((hid, rows), BF16), V((2 * tile, tile), F32),
            V((8, 8, tile), F32), V((8, 8, tile), F32), V((4, 1, 256), F32),
            dma((17,)), dma((4,)), dma((4,)), dma((32,)), dma((32,)), dma((32,)), dma((32,)),
            dma((4,)), dma((4,)), dma((3,)), dma((3,)), dma((2,)), dma((2,)), dma((8,)), dma((8,)),
        ],
        compiler_params=pltpu.CompilerParams(
            collective_id=0, has_side_effects=True, vmem_limit_bytes=64_500_000
        ),
    )(clip_groups, attn_query, attn_key, attn_value, attn_outgrad, fast_query, fast_outgrad, fast_key,
      gate_weights, up_weights, down_weights, gate_factor)
    outs = pl.pallas_call(
        put_out,
        out_shape=tuple(jax.ShapeDtypeStruct(o.shape, o.dtype) for o in outs),
        in_specs=[pl.BlockSpec(memory_space=V)] * 5,
        out_specs=(any_spec,) * 5,
        scratch_shapes=[dma((5,))],
        compiler_params=pltpu.CompilerParams(vmem_limit_bytes=1024 * 1024),
    )(*outs)
    return outs[0], outs[1], outs[2], outs[3], outs[4].reshape(tile)


def solution(mesh):
    both = ("tm", "space")
    return jax.shard_map(
        per_device,
        mesh=mesh,
        in_specs=(
            P(both, None), P(both, None), P(both, None), P(both, None),
            P("tm", None), P("tm", None), P("tm", None),
            P("tm", None, "space"), P("tm", None, "space"), P("tm", "space", None),
            P("tm", "space"), P(),
        ),
        out_specs=(P(both, None), P(both, None), P(both, None), P(both, None), P(both)),
        check_vma=False,
    )
```

time: 66.2 us -> 55.7 us (0.84)
  local copies, waits for them, and re-layouts: 7.21 us -> 0 us
  Pallas kernels: 58.1 us -> 54.9 us
    unnamed x9 -> x0, local copies, waits for them, and re-layouts: 7.21 us -> none
    pallas_call x1 -> x2, Pallas kernels: 58.1 us -> 54.9 us  [the longest x1 53.5 us: per_device(): pl.pallas_call(kernel, out_shape=(V((tile, width), BF16), V((tile, width)...]
where the time goes in v2:
time: 55.7 us; the launch traced here: 55.5 us
  Pallas kernels  54.9 us (99%)
  between operations  0.64 us (1%)
    pallas_call x1, Pallas kernels, per_device(): pl.pallas_call(kernel, out_shape=(V((tile, width), BF16), V((tile, width)...  53.5 us
    pallas_call x1, Pallas kernels, per_device(): pl.pallas_call(put_out, out_shape=tuple((jax.ShapeDtypeStruct(o.shape, o....  1.44 us

profile of v2, /device:TPU:1, one launch (start us, length us, event | category | flops | bytes accessed | tf_op | source)
XLA Modules:
  0.0 55.5 jit_solution(11267406812434543980)
XLA Ops:
  0.6 53.5 %shard_map.155 = (bf16[128,2560]{1,0:T(8,128)(2,1)S(1)}, bf16[128,2560]{1,0:T(8,128)(2,1)S(1)}, bf16[128,2560]{1,0:T(8,128)(2,1)S(1)}, bf16[128,1536]{1,0:T(8,128)(2,1)S(1)}, f32[1,128]{1,0:T(1,128)S(1)}) custom-call(s32[4]{0:T(128)} %clips.1, bf16[128,2560]{1,0:T(8,128)(2,1)} %aq.1, bf16[128,2560]{1,0:T(8,128)(2,1)} %ak.1, bf16[128,2560]{1,0:T(8,128)(2,1)} %av.1, ...), custom_call_target="tpu_custom_call" | custom-call | tf_op jit(solution)/shard_map/pallas_call | solution.py:358
  54.1 1.4 %shard_map.156 = (bf16[128,2560]{1,0:T(8,128)(2,1)}, bf16[128,2560]{1,0:T(8,128)(2,1)}, bf16[128,2560]{1,0:T(8,128)(2,1)}, bf16[128,1536]{1,0:T(8,128)(2,1)}, f32[1,128]{1,0:T(1,128)}) custom-call(bf16[128,2560]{1,0:T(8,128)(2,1)S(1)} %get-tuple-element.15.a, bf16[128,2560]{1,0:T(8,128)(2,1)S(1)} %get-tuple-element.16.b, ...), custom_call_target="tpu_custom_call" | custom-call | tf_op jit(solution)/shard_map/pallas_call | solution.py:385

commit v3 on v2

--- a/solution.py
+++ b/solution.py
@@ -10,7 +10,7 @@
 
 MESH = pl.DeviceIdType.MESH
 F32 = jnp.float32
-UNROLL = 2
+UNROLL = 5
 BF16 = jnp.bfloat16
 
 HEAD = 128
@@ -91,9 +91,6 @@
         halo(2, ak.at[pl.ds(tile - REACH, REACH)], kx.at[pl.ds(0, REACH)], right),
         halo(3, av.at[pl.ds(tile - REACH, REACH)], vx.at[pl.ds(0, REACH)], right),
     ]
-    pl.semaphore_wait(barrier, 22)
-    for c in halos:
-        c.start()
 
     def peer(kk):
         dz, dy = kk // 4, kk % 4
@@ -136,7 +133,11 @@
         g_t[:, at] = g.T
         return 0
 
-    lax.fori_loop(0, rows // rt, rows_step, 0)
+    lax.fori_loop(0, 2, rows_step, 0)
+    pl.semaphore_wait(barrier, 22)
+    for c in halos:
+        c.start()
+    lax.fori_loop(2, rows // rt, rows_step, 0)
     for c in later:
         c.start()
 
@@ -249,21 +250,21 @@
 
     steps = aq.shape[1] // HEAD // UNROLL
     lax.fori_loop(0, steps // 2, head_step, 0)
+    carries(0)
+    lax.fori_loop(steps // 2, steps, head_step, 0)
+
+    def back(i, to):
+        return pltpu.make_async_remote_copy(
+            src_ref=dkv_s.at[i], dst_ref=dkv_r.at[i], send_sem=dk_s.at[i], recv_sem=dk_r.at[i],
+            device_id={"space": to}, device_id_type=MESH,
+        )
+
+    backs = [back(0, left), back(1, right)]
+    for c in backs:
+        c.start()
     relay[0].wait_recv()
     psum[1] = (pair_sum(ahead) + rsx[0].astype(F32)).astype(BF16)
     relay[1].start()
-    carries(0)
-    lax.fori_loop(steps // 2, steps, head_step, 0)
-
-    def back(i, to):
-        return pltpu.make_async_remote_copy(
-            src_ref=dkv_s.at[i], dst_ref=dkv_r.at[i], send_sem=dk_s.at[i], recv_sem=dk_r.at[i],
-            device_id={"space": to}, device_id_type=MESH,
-        )
-
-    backs = [back(0, left), back(1, right)]
-    for c in backs:
-        c.start()
 
     for c in later[4:]:
         c.wait()
@@ -276,6 +277,31 @@
     lax.fori_loop(0, rows // rt, turn_step, 0)
 
     carries(1)
+
+    def rate_copy(d):
+        j = lax.rem(d - sp + 8, 8)
+        return pltpu.make_async_remote_copy(
+            src_ref=rate_s.at[d], dst_ref=rate_r.at[j], send_sem=rt_s.at[j], recv_sem=rt_r.at[j],
+            device_id={"space": d}, device_id_type=MESH,
+        )
+
+    def rate_part(n, r):
+        at = block(r)
+        kc = lax.dot_general(cin[n], k_b[at, pl.ds(n * half, half)], NT, preferred_element_type=F32)
+        return jnp.sum(kc * f_t[:, at].astype(F32), axis=0, keepdims=True)
+
+    def rate_first(r, _):
+        line[r] = rate_part(0, r)
+        return 0
+
+    def rate_second(r):
+        whole = (line[r] + rate_part(1, r)) * (1.0 / rows)
+        rate_s[2 * r] = jnp.broadcast_to(whole[:, :tile], (8, tile))
+        rate_s[2 * r + 1] = jnp.broadcast_to(whole[:, tile:], (8, tile))
+
+    for kk in ORDER:
+        carry_copy(0, kk).wait_recv()
+    lax.fori_loop(0, rows // rt, rate_first, 0)
 
     total = pair_sum(0)
     for i in (2, 1):
@@ -290,36 +316,22 @@
     o_v[pl.ds(0, REACH), :] = (dv_f[pl.ds(0, REACH), :] + dkv_r[1, 1].astype(F32)).astype(BF16)
     o_v[pl.ds(tile - REACH, REACH), :] = (dv_f[pl.ds(tile - REACH, REACH), :] + dkv_r[0, 1].astype(F32)).astype(BF16)
 
-    for n in range(2):
-        for kk in ORDER:
-            carry_copy(n, kk).wait_recv()
-
-        def rate_step(r, _, n=n):
-            at = block(r)
-            kc = lax.dot_general(cin[n], k_b[at, pl.ds(n * half, half)], NT, preferred_element_type=F32)
-            more = jnp.sum(kc * f_t[:, at].astype(F32), axis=0, keepdims=True)
-            if n == 0:
-                line[r] = more
-            else:
-                more = (line[r] + more) * (1.0 / rows)
-                rate_s[2 * r] = jnp.broadcast_to(more[:, :tile], (8, tile))
-                rate_s[2 * r + 1] = jnp.broadcast_to(more[:, tile:], (8, tile))
-            return 0
-
-        lax.fori_loop(0, rows // rt, rate_step, 0)
-
-    def rate_copy(j):
-        d = lax.rem(sp + j, 8)
-        return pltpu.make_async_remote_copy(
-            src_ref=rate_s.at[d], dst_ref=rate_r.at[j], send_sem=rt_s.at[j], recv_sem=rt_r.at[j],
-            device_id={"space": d}, device_id_type=MESH,
-        )
-
-    for j in range(1, 8):
-        rate_copy(j).start()
+    for kk in ORDER:
+        carry_copy(1, kk).wait_recv()
+
+    def rate_away(i):
+        r = lax.rem(mx + 2 + i, 4)
+        rate_second(r)
+        rate_copy(2 * r).start()
+        rate_copy(2 * r + 1).start()
+
+    for i in (0, 1, 3):
+        rate_away(i)
+    rate_second(mx)
+    rate_copy(2 * mx + 1 - mk).start()
     rate = rate_s[sp]
     for j in range(1, 8):
-        rate_copy(j).wait_recv()
+        rate_copy(lax.rem(sp + j, 8)).wait_recv()
         rate = rate + rate_r[j]
     o_r[...] = rate[0:1, :]
 
@@ -334,7 +346,7 @@
     for c in backs:
         c.wait_send()
     for j in range(1, 8):
-        rate_copy(j).wait_send()
+        rate_copy(lax.rem(sp + j, 8)).wait_send()
 
 
 def put_out(a, b, c, d, e, oa, ob, oc, od, oe, sem):

time: 55.7 us -> 52.1 us (0.935)
  Pallas kernels: 54.9 us -> 51.3 us
    pallas_call x1, Pallas kernels: 53.5 us -> 49.9 us  [per_device(): pl.pallas_call(kernel, out_shape=(V((tile, width), BF16), V((tile, width)...]
where the time goes in v3:
time: 52.1 us; the launch traced here: 52 us
  Pallas kernels  51.3 us (98%)
  between operations  0.64 us (1%)
    pallas_call x1, Pallas kernels, per_device(): pl.pallas_call(kernel, out_shape=(V((tile, width), BF16), V((tile, width)...  49.9 us
    pallas_call x1, Pallas kernels, per_device(): pl.pallas_call(put_out, out_shape=tuple((jax.ShapeDtypeStruct(o.shape, o....  1.44 us

profile of v3, /device:TPU:1, one launch (start us, length us, event | category | flops | bytes accessed | tf_op | source)
XLA Modules:
  0.0 52.0 jit_solution(2976018053422435805)
XLA Ops:
  0.6 49.9 %shard_map.155 = (bf16[128,2560]{1,0:T(8,128)(2,1)S(1)}, bf16[128,2560]{1,0:T(8,128)(2,1)S(1)}, bf16[128,2560]{1,0:T(8,128)(2,1)S(1)}, bf16[128,1536]{1,0:T(8,128)(2,1)S(1)}, f32[1,128]{1,0:T(1,128)S(1)}) custom-call(s32[4]{0:T(128)} %clips.1, bf16[128,2560]{1,0:T(8,128)(2,1)} %aq.1, bf16[128,2560]{1,0:T(8,128)(2,1)} %ak.1, bf16[128,2560]{1,0:T(8,128)(2,1)} %av.1, ...), custom_call_target="tpu_custom_call" | custom-call | tf_op jit(solution)/shard_map/pallas_call | solution.py:370
  50.5 1.4 %shard_map.156 = (bf16[128,2560]{1,0:T(8,128)(2,1)}, bf16[128,2560]{1,0:T(8,128)(2,1)}, bf16[128,2560]{1,0:T(8,128)(2,1)}, bf16[128,1536]{1,0:T(8,128)(2,1)}, f32[1,128]{1,0:T(1,128)}) custom-call(bf16[128,2560]{1,0:T(8,128)(2,1)S(1)} %get-tuple-element.15.a, bf16[128,2560]{1,0:T(8,128)(2,1)S(1)} %get-tuple-element.16.b, ...), custom_call_target="tpu_custom_call" | custom-call | tf_op jit(solution)/shard_map/pallas_call | solution.py:397

commit v4 on v3

--- a/solution.py
+++ b/solution.py
@@ -17,14 +17,14 @@
 REACH = 64
 NT = (((1,), (1,)), ((), ()))
 TN = (((0,), (0,)), ((), ()))
-ORDER = (10, 2, 8, 6, 14, 9, 11, 5, 15, 7, 13, 1, 3, 4, 12)
+ORDER = (10, 5, 15, 7, 13, 6, 9, 14, 11, 2, 8, 1, 4, 3, 12)
 
 
 def kernel(
     clips, aq, ak, av, ao, fq, fo, fk, wg, wu, wd, gf,
     o_q, o_k, o_v, o_f, o_r,
     q_b, o_b, k_b, w_b, wd_b, f_b, aq_b, ao_b, kx, vx,
-    gu, g_t, gtot, rx, cout, cin, ip, prx, psum, rsx,
+    gu, g_t, gtot0, gtot1, rx0, rx1, cout0, cout1, cin0, cin1, ip, prx, psum, rsx,
     dk_f, dv_f, dkv_s, dkv_r, f_t, bias, rate_s, rate_r, line,
     ld, halo_s, halo_r, a1_s, a1_r, a2_s, a2_r, pr_s, pr_r, rs_s, rs_r, dk_s, dk_r, rt_s, rt_r,
 ):
@@ -35,8 +35,8 @@
     feat = fq.shape[1]
     half = feat // 2
     tile = aq.shape[0]
-    blk = hid // 8
-    quarter = half // 2
+    parts, starts_at = (2 * hid // 3, hid // 3), (0, 2 * hid // 3)
+    gtot, rx, cout, cin = (gtot0, gtot1), (rx0, rx1), (cout0, cout1), (cin0, cin1)
     rt = 256
 
     barrier = pltpu.get_barrier_semaphore()
@@ -48,32 +48,34 @@
     def load(i, src, dst):
         return pltpu.make_async_copy(src, dst, ld.at[i])
 
-    weights = [
-        load(0, wg.at[0], w_b.at[:, pl.ds(0, hid)]),
-        load(1, wu.at[0], w_b.at[:, pl.ds(hid, hid)]),
-        load(2, wd.at[0], wd_b),
-    ]
+    def weights(n):
+        mine = pl.ds(starts_at[n], parts[n])
+        return [
+            load(3 * n, wg.at[0, :, mine], w_b.at[:, pl.ds(2 * starts_at[n], parts[n])]),
+            load(3 * n + 1, wu.at[0, :, mine], w_b.at[:, pl.ds(2 * starts_at[n] + parts[n], parts[n])]),
+            load(3 * n + 2, wd.at[0, mine], wd_b.at[mine]),
+        ]
 
     def block(r):
         return pl.ds(pl.multiple_of(r * rt, rt), rt)
 
     def inputs(r):
         return [
-            load(3 + r, fq.at[block(r)], q_b.at[block(r)]),
-            load(7 + r, fo.at[block(r)], o_b.at[block(r)]),
+            load(6 + r, fq.at[block(r)], q_b.at[block(r)]),
+            load(10 + r, fo.at[block(r)], o_b.at[block(r)]),
         ]
 
     later = [
-        load(11, aq, aq_b),
-        load(12, ao, ao_b),
-        load(13, ak, kx.at[pl.ds(REACH, tile)]),
-        load(14, av, vx.at[pl.ds(REACH, tile)]),
-        load(15, fk, k_b),
-        load(16, gf, f_b),
+        load(14, aq, aq_b),
+        load(15, ao, ao_b),
+        load(16, ak, kx.at[pl.ds(REACH, tile)]),
+        load(17, av, vx.at[pl.ds(REACH, tile)]),
+        load(18, fk, k_b),
+        load(19, gf, f_b),
     ]
-    for c in weights:
+    for c in weights(0):
         c.start()
-    for r in range(4):
+    for r in range(2):
         for c in inputs(r):
             c.start()
 
@@ -96,14 +98,15 @@
         dz, dy = kk // 4, kk % 4
         return lax.rem(mz + dz, 4) * 4 + lax.rem(my + dy, 4)
 
-    def slice_of(ref, n, d):
-        down, over = pl.multiple_of((d // 2) * blk, 16), pl.multiple_of(lax.rem(d, 2) * quarter, 128)
-        return ref.at[n, pl.ds(down, blk), pl.ds(over, quarter)]
+    def slice_of(refs, n, d):
+        blk = parts[n] // 8
+        down, over = pl.multiple_of((d // 2) * blk, 16), pl.multiple_of(lax.rem(d, 2) * half, 128)
+        return refs[n].at[pl.ds(down, blk), pl.ds(over, half)]
 
     def out_copy(n, kk):
         d = peer(kk)
         return pltpu.make_async_remote_copy(
-            src_ref=slice_of(gtot, n, d), dst_ref=rx.at[n, tm],
+            src_ref=slice_of(gtot, n, d), dst_ref=rx[n].at[tm],
             send_sem=a1_s.at[n * 16 + kk], recv_sem=a1_r.at[n * 16 + kk],
             device_id={"tm": d}, device_id_type=MESH,
         )
@@ -111,47 +114,56 @@
     def carry_copy(n, kk):
         d = peer(kk)
         return pltpu.make_async_remote_copy(
-            src_ref=cout.at[n, d], dst_ref=slice_of(cin, n, tm),
+            src_ref=cout[n].at[d], dst_ref=slice_of(cin, n, tm),
             send_sem=a2_s.at[n * 16 + kk], recv_sem=a2_r.at[n * 16 + kk],
             device_id={"tm": d}, device_id_type=MESH,
         )
 
-    for c in weights:
-        c.wait()
-
-    def rows_step(r, _):
-        at = block(r)
-        for c in inputs(r):
+    for n in range(2):
+        part, off = parts[n], starts_at[n]
+        for c in weights(n):
             c.wait()
-        pre = jnp.dot(q_b[at, :], w_b[...], preferred_element_type=F32)
-        hg = lax.dot_general(o_b[at, :], wd_b[...], NT, preferred_element_type=F32)
-        gate, up = pre[:, :hid], pre[:, hid:]
-        sig = 1.0 / (1.0 + jnp.exp(-gate))
-        g = (hg * up * sig * (1.0 + gate * (1.0 - sig))).astype(BF16)
-        gu[at, pl.ds(0, hid)] = g
-        gu[at, pl.ds(hid, hid)] = (hg * (gate * sig)).astype(BF16)
-        g_t[:, at] = g.T
-        return 0
-
-    lax.fori_loop(0, 2, rows_step, 0)
-    pl.semaphore_wait(barrier, 22)
-    for c in halos:
-        c.start()
-    lax.fori_loop(2, rows // rt, rows_step, 0)
-    for c in later:
-        c.start()
-
-    for n in range(2):
-        def total_step(i, _, n=n):
+        if n == 0:
+            for r in range(2, 4):
+                for c in inputs(r):
+                    c.start()
+            for c in weights(1):
+                c.start()
+
+        def rows_step(r, _, n=n, part=part, off=off):
+            at = block(r)
+            if n == 0:
+                for c in inputs(r):
+                    c.wait()
+            pre = jnp.dot(q_b[at, :], w_b[:, pl.ds(2 * off, 2 * part)], preferred_element_type=F32)
+            hg = lax.dot_general(o_b[at, :], wd_b[pl.ds(off, part), :], NT, preferred_element_type=F32)
+            gate, up = pre[:, :part], pre[:, part:]
+            sig = 1.0 / (1.0 + jnp.exp(-gate))
+            g = (hg * up * sig * (1.0 + gate * (1.0 - sig))).astype(BF16)
+            gu[at, pl.ds(2 * off, part)] = g
+            gu[at, pl.ds(2 * off + part, part)] = (hg * (gate * sig)).astype(BF16)
+            g_t[pl.ds(off, part), at] = g.T
+            return 0
+
+        lax.fori_loop(0, rows // rt, rows_step, 0)
+        if n == 0:
+            for c in later:
+                c.start()
+
+        def total_step(i, _, n=n, part=part, off=off):
             at = pl.ds(pl.multiple_of(i * 256, 256), 256)
-            src = pl.ds(pl.multiple_of(n * half + i * 256, 256), 256)
-            gtot[n, :, at] = jnp.dot(g_t[...], q_b[:, src], preferred_element_type=F32).astype(BF16)
+            total = jnp.dot(g_t[pl.ds(off, part), :], q_b[:, at], preferred_element_type=F32)
+            gtot[n][:, at] = total.astype(BF16)
             return 0
 
-        lax.fori_loop(0, half // 256, total_step, 0)
+        lax.fori_loop(0, feat // 256, total_step, 0)
+        if n == 0:
+            pl.semaphore_wait(barrier, 22)
+            for c in halos:
+                c.start()
         for kk in ORDER:
             out_copy(n, kk).start()
-        rx[n, tm] = slice_of(gtot, n, tm)[...]
+        rx[n][tm] = slice_of(gtot, n, tm)[...]
 
     s1 = clips[0]
     s2 = s1 + clips[1]
@@ -163,15 +175,15 @@
 
         def scan_step(i, carry):
             c = 15 - i
-            cout[n, c] = carry.astype(BF16)
+            cout[n][c] = carry.astype(BF16)
             starts = (c == 0) | (c == s1) | (c == s2) | (c == s3)
             keep = jnp.where(starts, 0.0, 1.0).astype(F32)
-            return keep * (carry + rx[n, c].astype(F32))
-
-        lax.fori_loop(0, 16, scan_step, jnp.zeros((blk, quarter), F32))
+            return keep * (carry + rx[n][c].astype(F32))
+
+        lax.fori_loop(0, 16, scan_step, jnp.zeros((parts[n] // 8, half), F32))
         for kk in ORDER:
             carry_copy(n, kk).start()
-        slice_of(cin, n, tm)[...] = cout[n, tm]
+        slice_of(cin, n, tm)[...] = cout[n][tm]
 
     def partner_copy(x):
         return pltpu.make_async_remote_copy(
@@ -262,9 +274,6 @@
     backs = [back(0, left), back(1, right)]
     for c in backs:
         c.start()
-    relay[0].wait_recv()
-    psum[1] = (pair_sum(ahead) + rsx[0].astype(F32)).astype(BF16)
-    relay[1].start()
 
     for c in later[4:]:
         c.wait()
@@ -277,6 +286,9 @@
     lax.fori_loop(0, rows // rt, turn_step, 0)
 
     carries(1)
+    relay[0].wait_recv()
+    psum[1] = (pair_sum(ahead) + rsx[0].astype(F32)).astype(BF16)
+    relay[1].start()
 
     def rate_copy(d):
         j = lax.rem(d - sp + 8, 8)
@@ -287,8 +299,9 @@
 
     def rate_part(n, r):
         at = block(r)
-        kc = lax.dot_general(cin[n], k_b[at, pl.ds(n * half, half)], NT, preferred_element_type=F32)
-        return jnp.sum(kc * f_t[:, at].astype(F32), axis=0, keepdims=True)
+        kc = lax.dot_general(cin[n][...], k_b[at, :], NT, preferred_element_type=F32)
+        factors = f_t[pl.ds(starts_at[n], parts[n]), at].astype(F32)
+        return jnp.sum(kc * factors, axis=0, keepdims=True)
 
     def rate_first(r, _):
         line[r] = rate_part(0, r)
@@ -363,7 +376,8 @@
     tile, width = attn_query.shape
     rows, hid = gate_factor.shape
     feat = fast_query.shape[1]
-    half, blk = feat // 2, hid // 8
+    half, third = feat // 2, hid // 3
+    blk = third // 8
     any_spec = pl.BlockSpec(memory_space=pl.ANY)
     dma = pltpu.SemaphoreType.DMA
     V = pltpu.VMEM
@@ -379,14 +393,15 @@
             V((rows, feat), BF16), V((rows, feat), BF16), V((rows, feat), BF16),
             V((feat, 2 * hid), BF16), V((hid, feat), BF16), V((rows, hid), BF16),
             V((tile, width), BF16), V((tile, width), BF16), V((2 * tile, width), BF16), V((2 * tile, width), BF16),
-            V((rows, 2 * hid), BF16), V((hid, rows), BF16), V((2, hid, half), BF16),
-            V((2, 16, blk, half // 2), BF16), V((2, 16, blk, half // 2), BF16), V((2, hid, half), BF16),
+            V((rows, 2 * hid), BF16), V((hid, rows), BF16), V((2 * third, feat), BF16), V((third, feat), BF16),
+            V((16, 2 * blk, half), BF16), V((16, blk, half), BF16), V((16, 2 * blk, half), BF16), V((16, blk, half), BF16),
+            V((2 * third, feat), BF16), V((third, feat), BF16),
             V((rows, feat), BF16), V((4, tile, feat), BF16), V((3, tile, feat), BF16), V((3, tile, feat), BF16),
             V((tile, width), F32), V((tile, width), F32),
             V((2, 2, REACH, width), BF16), V((2, 2, REACH, width), BF16),
             V((hid, rows), BF16), V((2 * tile, tile), F32),
             V((8, 8, tile), F32), V((8, 8, tile), F32), V((4, 1, 256), F32),
-            dma((17,)), dma((4,)), dma((4,)), dma((32,)), dma((32,)), dma((32,)), dma((32,)),
+            dma((20,)), dma((4,)), dma((4,)), dma((32,)), dma((32,)), dma((32,)), dma((32,)),
             dma((4,)), dma((4,)), dma((3,)), dma((3,)), dma((2,)), dma((2,)), dma((8,)), dma((8,)),
         ],
         compiler_params=pltpu.CompilerParams(

time: 52.1 us -> 51.2 us (0.983)
  Pallas kernels: 51.3 us -> 50.5 us
    pallas_call x1, Pallas kernels: 49.9 us -> 49 us  [per_device(): pl.pallas_call(kernel, out_shape=(V((tile, width), BF16), V((tile, width)...]
where the time goes in v4:
time: 51.2 us; the launch traced here: 51.1 us
  Pallas kernels  50.5 us (99%)
  between operations  0.64 us (1%)
    pallas_call x1, Pallas kernels, per_device(): pl.pallas_call(kernel, out_shape=(V((tile, width), BF16), V((tile, width)...  49 us
    pallas_call x1, Pallas kernels, per_device(): pl.pallas_call(put_out, out_shape=tuple((jax.ShapeDtypeStruct(o.shape, o....  1.44 us

profile of v4, /device:TPU:1, one launch (start us, length us, event | category | flops | bytes accessed | tf_op | source)
XLA Modules:
  0.0 51.1 jit_solution(5852546716080945691)
XLA Ops:
  0.6 49.0 %shard_map.155 = (bf16[128,2560]{1,0:T(8,128)(2,1)S(1)}, bf16[128,2560]{1,0:T(8,128)(2,1)S(1)}, bf16[128,2560]{1,0:T(8,128)(2,1)S(1)}, bf16[128,1536]{1,0:T(8,128)(2,1)S(1)}, f32[1,128]{1,0:T(1,128)S(1)}) custom-call(s32[4]{0:T(128)} %clips.1, bf16[128,2560]{1,0:T(8,128)(2,1)} %aq.1, bf16[128,2560]{1,0:T(8,128)(2,1)} %ak.1, bf16[128,2560]{1,0:T(8,128)(2,1)} %av.1, ...), custom_call_target="tpu_custom_call" | custom-call | tf_op jit(solution)/shard_map/pallas_call | solution.py:384
  49.7 1.4 %shard_map.156 = (bf16[128,2560]{1,0:T(8,128)(2,1)}, bf16[128,2560]{1,0:T(8,128)(2,1)}, bf16[128,2560]{1,0:T(8,128)(2,1)}, bf16[128,1536]{1,0:T(8,128)(2,1)}, f32[1,128]{1,0:T(1,128)}) custom-call(bf16[128,2560]{1,0:T(8,128)(2,1)S(1)} %get-tuple-element.15.a, bf16[128,2560]{1,0:T(8,128)(2,1)S(1)} %get-tuple-element.16.b, ...), custom_call_target="tpu_custom_call" | custom-call | tf_op jit(solution)/shard_map/pallas_call | solution.py:412

commit v5 on v4

--- a/solution.py
+++ b/solution.py
@@ -10,7 +10,7 @@
 
 MESH = pl.DeviceIdType.MESH
 F32 = jnp.float32
-UNROLL = 5
+UNROLL = 10
 BF16 = jnp.bfloat16
 
 HEAD = 128
@@ -363,8 +363,11 @@
 
 
 def put_out(a, b, c, d, e, oa, ob, oc, od, oe, sem):
-    copies = [pltpu.make_async_copy(src, dst, sem.at[i])
-              for i, (src, dst) in enumerate(((a, oa), (b, ob), (c, oc), (d, od), (e, oe)))]
+    pairs = [(d, od), (e, oe)]
+    for src, dst in ((a, oa), (b, ob), (c, oc)):
+        rows = src.shape[0] // 4
+        pairs += [(src.at[pl.ds(i * rows, rows)], dst.at[pl.ds(i * rows, rows)]) for i in range(4)]
+    copies = [pltpu.make_async_copy(src, dst, sem.at[i]) for i, (src, dst) in enumerate(pairs)]
     for c in copies:
         c.start()
     for c in copies:
@@ -414,7 +417,7 @@
         out_shape=tuple(jax.ShapeDtypeStruct(o.shape, o.dtype) for o in outs),
         in_specs=[pl.BlockSpec(memory_space=V)] * 5,
         out_specs=(any_spec,) * 5,
-        scratch_shapes=[dma((5,))],
+        scratch_shapes=[dma((14,))],
         compiler_params=pltpu.CompilerParams(vmem_limit_bytes=1024 * 1024),
     )(*outs)
     return outs[0], outs[1], outs[2], outs[3], outs[4].reshape(tile)

time: 51.2 us -> 51.2 us (level)
  no operation moved by 1% of the time
where the time goes in v5:
time: 51.2 us; the launch traced here: 51.1 us
  Pallas kernels  50.5 us (99%)
  between operations  0.64 us (1%)
    pallas_call x1, Pallas kernels, per_device(): pl.pallas_call(kernel, out_shape=(V((tile, width), BF16), V((tile, width)...  48.9 us
    pallas_call x1, Pallas kernels, per_device(): pl.pallas_call(put_out, out_shape=tuple((jax.ShapeDtypeStruct(o.shape, o....  1.52 us

profile of v5, /device:TPU:1, one launch (start us, length us, event | category | flops | bytes accessed | tf_op | source)
XLA Modules:
  0.0 51.1 jit_solution(11988677980280929156)
XLA Ops:
  0.6 48.9 %shard_map.155 = (bf16[128,2560]{1,0:T(8,128)(2,1)S(1)}, bf16[128,2560]{1,0:T(8,128)(2,1)S(1)}, bf16[128,2560]{1,0:T(8,128)(2,1)S(1)}, bf16[128,1536]{1,0:T(8,128)(2,1)S(1)}, f32[1,128]{1,0:T(1,128)S(1)}) custom-call(s32[4]{0:T(128)} %clips.1, bf16[128,2560]{1,0:T(8,128)(2,1)} %aq.1, bf16[128,2560]{1,0:T(8,128)(2,1)} %ak.1, bf16[128,2560]{1,0:T(8,128)(2,1)} %av.1, ...), custom_call_target="tpu_custom_call" | custom-call | tf_op jit(solution)/shard_map/pallas_call | solution.py:387
  49.6 1.5 %shard_map.156 = (bf16[128,2560]{1,0:T(8,128)(2,1)}, bf16[128,2560]{1,0:T(8,128)(2,1)}, bf16[128,2560]{1,0:T(8,128)(2,1)}, bf16[128,1536]{1,0:T(8,128)(2,1)}, f32[1,128]{1,0:T(1,128)}) custom-call(bf16[128,2560]{1,0:T(8,128)(2,1)S(1)} %get-tuple-element.15.a, bf16[128,2560]{1,0:T(8,128)(2,1)S(1)} %get-tuple-element.16.b, ...), custom_call_target="tpu_custom_call" | custom-call | tf_op jit(solution)/shard_map/pallas_call | solution.py:415
